TPU v7x, 512 devices: a whole 4x8x8 slice. The times are simulated.
512 devices in a mesh: tx: 32 (over z_lo, y, core), ty: 16 (over z_hi, x).
Axes of the slice: x: 4, y: 8, z: 8 (z_hi: 4, z_lo: 2; z = z_hi * 2 + z_lo), core: 2. Of those that a mesh axis runs over, the one named last changes fastest.
Arguments:
- nodes: bfloat16 [256, 256, 512], P('tx', 'ty'), may hold values from -6 to 6
- edges: bfloat16 [32, 16, 1024, 512], P('tx', 'ty'), may hold values from -6 to 6
- edge_sender: int32 [32, 16, 1024], P('tx', 'ty'), may hold values from 0 to 224, as said below
- edge_receiver: int32 [32, 16, 1024], P('tx', 'ty'), may hold values from 0 to 128, as said below
- coarse_place: int32 [2560], P(('tx', 'ty')), may hold values from 0 to 127, as said below
- edge_w1: bfloat16 [1536, 512], replicated, may hold values from -0.15625 to 0.15625
- edge_w2: bfloat16 [512, 512], replicated, may hold values from -0.25 to 0.25
- edge_gain: float32 [512], replicated, may hold values from 0.1 to 1.9
- node_w1: bfloat16 [1024, 512], replicated, may hold values from -0.1875 to 0.1875
- node_w2: bfloat16 [512, 512], replicated, may hold values from -0.25 to 0.25
- node_gain: float32 [512], replicated, may hold values from 0.1 to 1.9
Outputs:
- new_nodes: bfloat16 [256, 256, 512], P('tx', 'ty')
- new_edges: bfloat16 [32, 16, 1024, 512], P('tx', 'ty')
Inputs may be any that keep to these rules, and one draw needn't show every extreme that they name: `edge_sender`: entries below 180 index the tile extended by one node on each side, wrapping around the grid, row-major over (10) x (18); entries from 180 on name a coarse node of the tile or of one of the eight tiles around it, as the steps say. `edge_receiver`: entry 128 marks an empty slot; on each tile the live slots come first, and at least three quarters of the slots are live. A live slot whose sender entry is 180 or more has as receiver one of the tile's own coarse nodes. `coarse_place`: the 5 entries of one tile are distinct.
All inputs are finite; a program needn't handle non-finite values.
Results may differ from a plain program's by a relative error of at most 0.0056.
Values may be sent and summed in bfloat16 or wider, within the bound.
No kernel may reach another device: no remote copies, remote signals or barrier semaphores. Data moves between devices by JAX's collectives and lax.ppermute only.
A program may use at most 64 MiB of HBM per device.

v0:
```python
import jax
import jax.numpy as jnp
from jax import lax
from jax.sharding import PartitionSpec as P

eps = 1e-05


def extended(shard, sides, width):
    for axis, dim in sides:
        size, length = (lax.axis_size(axis), shard.shape[dim])
        up = [(i, (i + 1) % size) for i in range(size)]
        down = [(j, i) for i, j in up]
        last = lax.slice_in_dim(shard, length - width, length, axis=dim)
        leading = lax.slice_in_dim(shard, 0, width, axis=dim)
        before = lax.ppermute(last, axis, up)
        after = lax.ppermute(leading, axis, down)
        shard = jnp.concatenate([before, shard, after], axis=dim)
    return shard


def layer_norm(values, gain):
    average = jnp.mean(values, -1, keepdims=True)
    centred = values - average
    variance = jnp.mean(centred * centred, -1, keepdims=True)
    return centred * lax.rsqrt(variance + eps) * gain


def shards(
    nodes,
    edges,
    edge_sender,
    edge_receiver,
    coarse_place,
    edge_w1,
    edge_w2,
    edge_gain,
    node_w1,
    node_w2,
    node_gain,
):
    tile_rows, tile_cols, feature = nodes.shape
    node_rows = tile_rows * tile_cols
    node_flat = nodes.reshape(node_rows, feature)
    owned_count = coarse_place.shape[0]
    source = jnp.dot(
        node_flat, edge_w1[feature : 2 * feature], preferred_element_type=jnp.float32
    ).astype(jnp.bfloat16)
    coarse_own = jnp.take(source, coarse_place, axis=0)
    bordered = extended(source.reshape(tile_rows, tile_cols, feature), (("tx", 0), ("ty", 1)), 1)
    coarse_near = extended(
        coarse_own.reshape(1, 1, owned_count, feature), (("tx", 0), ("ty", 1)), 1
    )
    sources = jnp.concatenate([bordered.reshape(-1, feature), coarse_near.reshape(-1, feature)], 0)
    receiver_term = jnp.dot(
        node_flat, edge_w1[2 * feature :], preferred_element_type=jnp.float32
    ).astype(jnp.bfloat16)
    edge_flat = edges.reshape(-1, feature)
    send_flat = edge_sender.reshape(-1)
    recv_flat = edge_receiver.reshape(-1)
    picked = jnp.take(sources, send_flat, axis=0)
    sender = picked.astype(jnp.float32)
    landing = (recv_flat[:, None] == jnp.arange(node_rows, dtype=jnp.int32)[None, :]).astype(
        jnp.bfloat16
    )
    recv_rows = jnp.dot(landing, receiver_term, preferred_element_type=jnp.float32)
    preact = (
        jnp.dot(edge_flat, edge_w1[:feature], preferred_element_type=jnp.float32)
        + sender
        + recv_rows
    )
    hidden = jax.nn.silu(preact).astype(jnp.bfloat16)
    message = jnp.dot(hidden, edge_w2, preferred_element_type=jnp.float32)
    is_live = (recv_flat < node_rows)[:, None]
    normed = jnp.where(is_live, layer_norm(message, edge_gain), jnp.float32(0.0))
    updated = (edge_flat.astype(jnp.float32) + normed).astype(jnp.bfloat16)
    summed = lax.dot_general(
        landing, updated, (((0,), (0,)), ((), ())), preferred_element_type=jnp.float32
    ).astype(jnp.bfloat16)
    node_pre = jnp.dot(node_flat, node_w1[:feature], preferred_element_type=jnp.float32) + jnp.dot(
        summed, node_w1[feature:], preferred_element_type=jnp.float32
    )
    node_hidden = jax.nn.silu(node_pre).astype(jnp.bfloat16)
    node_out = jnp.dot(node_hidden, node_w2, preferred_element_type=jnp.float32)
    new_nodes = (node_flat.astype(jnp.float32) + layer_norm(node_out, node_gain)).astype(
        jnp.bfloat16
    )
    return (new_nodes.reshape(tile_rows, tile_cols, feature), updated.reshape(edges.shape))


def solution(mesh):
    placed = (
        P("tx", "ty", None),
        P("tx", "ty", None, None),
        P("tx", "ty", None),
        P("tx", "ty", None),
        P(("tx", "ty")),
        P(),
        P(),
        P(),
        P(),
        P(),
        P(),
    )
    return jax.shard_map(
        shards,
        mesh=mesh,
        in_specs=placed,
        out_specs=(P("tx", "ty", None), P("tx", "ty", None, None)),
        check_vma=False,
    )
```

profile of v0, /device:TPU:134, one launch (start us, length us, event | category | flops | bytes accessed | tf_op | source)
XLA Modules:
  0.0 70.2 jit_solution(5927282117591491451)
XLA Ops:
  0.6 0.0 copy-start
  0.6 0.0 copy-start.3
  0.7 0.0 copy-start.6
  0.7 0.0 copy-start.7
  0.7 0.7 %compare_select_fusion.2 = s32[5]{0:T(128)S(1)} fusion(s32[5]{0:T(128)} %param.15), kind=kLoop, calls=%fused_computation.44 | loop fusion | flops 15 | bytes 40 | tf_op jit(solution)/shard_map/jit(_take)/jit(_where)/select_n | solution.py:49
  1.4 0.7 compare_and_fusion.1
  2.1 1.3 %convolution_convert_fusion.1 = bf16[128,512]{1,0:T(8,128)(2,1)S(1)} fusion(bf16[128,512]{1,0:T(8,128)(2,1)} %bitcast.32, bf16[1536,512]{1,0:T(8,128)(2,1)} %param.16), kind=kOutput, calls=%fused_computation.8 | convolution fusion | flops 67174400 | bytes 786432 | tf_op jit(solution)/shard_map/dot_general | solution.py:46
  3.4 0.0 copy-start.4
  3.4 0.6 gather_fusion
  4.0 0.1 bitcast_select_fusion
  4.1 1.9 %collective-permute-start.4 = (bf16[1,1,5,512]{3,2,1,0:T(8,128)(2,1)S(1)}, bf16[1,1,5,512]{3,2,1,0:T(8,128)(2,1)S(1)}, u32[]{:S(2)}, u32[]{:S(2)}) collective-permute-start(bf16[1,1,5,512]{3,2,1,0:T(8,128)(2,1)S(1)} %bitcast_select_fusion), channel_id=1, source_target_pairs={{0,16},{16,32},{32,48},{48,64},{64,80},{80,96},{96,112},{112,128},... | collective-permute-start | bytes 15368 | tf_op jit(solution)/shard_map/ppermute | solution.py:16
  6.0 6.6 %collective-permute-start.5 = (bf16[1,1,5,512]{3,2,1,0:T(8,128)(2,1)S(1)}, bf16[1,1,5,512]{3,2,1,0:T(8,128)(2,1)S(1)}, u32[]{:S(2)}, u32[]{:S(2)}) collective-permute-start(bf16[1,1,5,512]{3,2,1,0:T(8,128)(2,1)S(1)} %bitcast_select_fusion), channel_id=1, source_target_pairs={{16,0},{32,16},{48,32},{64,48},{80,64},{96,80},{112,96},{128,112},... | collective-permute-start | bytes 15368 | tf_op jit(solution)/shard_map/ppermute | solution.py:17
  12.6 1.9 %collective-permute-start = (bf16[1,16,512]{2,1,0:T(8,128)(2,1)S(1)}, bf16[1,16,512]{2,1,0:T(8,128)(2,1)S(1)}, u32[]{:S(2)}, u32[]{:S(2)}) collective-permute-start(bf16[1,16,512]{2,1,0:T(8,128)(2,1)S(1)} %get-tuple-element.8), channel_id=1, source_target_pairs={{0,16},{16,32},{32,48},{48,64},{64,80},{80,96},{96,112},{112,128},... | collective-permute-start | bytes 49160 | tf_op jit(solution)/shard_map/ppermute | solution.py:16
  14.6 5.8 %collective-permute-start.1 = (bf16[1,16,512]{2,1,0:T(8,128)(2,1)S(1)}, bf16[1,16,512]{2,1,0:T(8,128)(2,1)S(1)}, u32[]{:S(2)}, u32[]{:S(2)}) collective-permute-start(bf16[1,16,512]{2,1,0:T(8,128)(2,1)S(1)} %get-tuple-element.9), channel_id=1, source_target_pairs={{16,0},{32,16},{48,32},{64,48},{80,64},{96,80},{112,96},{128,112},... | collective-permute-start | bytes 49160 | tf_op jit(solution)/shard_map/ppermute | solution.py:17
  20.3 3.1 %fusion.1 = f32[1024,512]{1,0:T(8,128)} fusion(bf16[128,512]{1,0:T(8,128)(2,1)} %bitcast.33, bf16[1536,512]{1,0:T(8,128)(2,1)} %param.16, s32[1024]{0:T(1024)} %bitcast.38), kind=kOutput, calls=%fused_computation.10 | convolution fusion | flops 201523200 | bytes 2756608 | tf_op jit(solution)/shard_map/dot_general | solution.py:66
  23.4 0.0 copy-done.6
  23.4 0.0 copy-done.7
  23.5 1.3 %fusion.15 = f32[128,512]{1,0:T(8,128)S(1)} fusion(bf16[128,512]{1,0:T(8,128)(2,1)S(1)} %bitcast.34, bf16[1024,512]{1,0:T(8,128)(2,1)} %param.19), kind=kOutput, calls=%fused_computation.22 | convolution fusion | flops 67108864 | bytes 917504 | tf_op jit(solution)/shard_map/dot_general | solution.py:80
  24.8 1.3 %copy.15 = bf16[1,1,1024,512]{2,3,1,0:T(8,128)(2,1)} copy(bf16[1,1,1024,512]{3,2,1,0:T(8,128)(2,1)S(1)} %copy-done.4) | data formatting | bytes 2097152 | tf_op args[1]
  26.1 0.0 collective-permute-done.4
  26.1 0.0 collective-permute-done.5
  26.1 6.3 %collective-permute-start.6 = (bf16[3,1,5,512]{3,2,1,0:T(8,128)(2,1)S(1)}, bf16[3,1,5,512]{3,2,1,0:T(8,128)(2,1)S(1)}, u32[]{:S(2)}, u32[]{:S(2)}) collective-permute-start(bf16[3,1,5,512]{3,2,1,0:T(8,128)(2,1)S(1)} %pad_maximum_fusion.3), channel_id=1, source_target_pairs={{0,1},{1,2},{2,3},{3,4},{4,5},{5,6},{6,7},{7,8},{8,9},{9,10},{10,1... | collective-permute-start | bytes 46088 | tf_op jit(solution)/shard_map/ppermute | solution.py:16
  32.5 1.9 %collective-permute-start.7 = (bf16[3,1,5,512]{3,2,1,0:T(8,128)(2,1)S(1)}, bf16[3,1,5,512]{3,2,1,0:T(8,128)(2,1)S(1)}, u32[]{:S(2)}, u32[]{:S(2)}) collective-permute-start(bf16[3,1,5,512]{3,2,1,0:T(8,128)(2,1)S(1)} %pad_maximum_fusion.3), channel_id=1, source_target_pairs={{1,0},{2,1},{3,2},{4,3},{5,4},{6,5},{7,6},{8,7},{9,8},{10,9},{11,1... | collective-permute-start | bytes 46088 | tf_op jit(solution)/shard_map/ppermute | solution.py:17
  34.4 0.0 collective-permute-done
  34.4 0.0 collective-permute-done.1
  34.5 8.1 %collective-permute-start.2 = (bf16[10,1,512]{2,1,0:T(2,128)(2,1)S(1)}, bf16[10,1,512]{2,1,0:T(2,128)(2,1)S(1)}, u32[]{:S(2)}, u32[]{:S(2)}) collective-permute-start(bf16[10,1,512]{2,1,0:T(2,128)(2,1)S(1)} %get-tuple-element.6), channel_id=1, source_target_pairs={{0,1},{1,2},{2,3},{3,4},{4,5},{5,6},{6,7},{7,8},{8,9},{9,10},{10,1... | collective-permute-start | bytes 30728 | tf_op jit(solution)/shard_map/ppermute | solution.py:16
  42.6 1.9 %collective-permute-start.3 = (bf16[10,1,512]{2,1,0:T(2,128)(2,1)S(1)}, bf16[10,1,512]{2,1,0:T(2,128)(2,1)S(1)}, u32[]{:S(2)}, u32[]{:S(2)}) collective-permute-start(bf16[10,1,512]{2,1,0:T(2,128)(2,1)S(1)} %get-tuple-element.7), channel_id=1, source_target_pairs={{1,0},{2,1},{3,2},{4,3},{5,4},{6,5},{7,6},{8,7},{9,8},{10,9},{11,1... | collective-permute-start | bytes 30728 | tf_op jit(solution)/shard_map/ppermute | solution.py:17
  44.6 0.0 collective-permute-done.6
  44.6 0.0 collective-permute-done.7
  44.6 0.0 collective-permute-done.2
  44.7 7.9 %collective-permute-done.3 = bf16[10,1,512]{2,1,0:T(2,128)(2,1)S(1)} collective-permute-done((bf16[10,1,512]{2,1,0:T(2,128)(2,1)S(1)}, bf16[10,1,512]{2,1,0:T(2,128)(2,1)S(1)}, u32[]{:S(2)}, u32[]{:S(2)}) %collective-permute-start.3) | collective-permute-done | bytes 10272 | tf_op jit(solution)/shard_map/ppermute | solution.py:17
  52.5 0.1 pad_maximum_fusion
  52.6 0.1 reshape.133
  52.7 5.1 %gather_fusion.1 = bf16[1024,512]{1,0:T(8,128)(2,1)} fusion(bf16[225,512]{1,0:T(8,128)(2,1)S(1)} %pad_maximum_fusion.1, s32[1024]{0:T(1024)S(1)} %broadcast_clamp_fusion), kind=kCustom, calls=%fused_computation.1 | custom fusion | bytes 2101248 | tf_op jit(solution)/shard_map/jit(_take)/gather | solution.py:61
  57.8 0.0 copy-done
  57.8 4.0 %fusion.28 = (f32[1024]{0:T(1024)S(1)}, f32[1024,512]{0,1:T(8,128)S(1)}) fusion(bf16[512,512]{1,0:T(8,128)(2,1)S(1)} %copy-done, f32[1024,512]{1,0:T(8,128)} %fusion.1, bf16[1,1,1024,512]{3,2,1,0:T(8,128)(2,1)} %param.12, bf16[1024,512]{1,0:T(8,128)(2,1)} %gather_fusion.1, pred[1024]{0:T(1024)(128)(4,1)S(1)} %compare_and_fusion, bf16[1536,512]{1,0:T(8,128)(2,1)} %param.16), kind=kOutput, calls=%fused_computation.53 | convolution fusion | flops 1078983680 | bytes 7345152 | tf_op jit(solution)/shard_map/dot_general | solution.py:73
  61.8 0.0 copy-start.8
  61.8 0.3 multiply_reduce_fusion
  62.1 0.9 %copy-done.1 = bf16[1,1,1024,512]{2,3,1,0:T(8,128)(2,1)S(1)} copy-done((bf16[1,1,1024,512]{2,3,1,0:T(8,128)(2,1)S(1)}, bf16[1,1,1024,512]{2,3,1,0:T(8,128)(2,1)}, u32[]{:S(2)}) %copy-start.1) | copy-done | bytes 1048600
  63.0 0.0 copy-done.8
  63.0 1.5 %add_convert_fusion = bf16[1024,512]{0,1:T(8,128)(2,1)} fusion(f32[1024,512]{0,1:T(8,128)S(1)} %get-tuple-element.11, bf16[1,1,1024,512]{2,3,1,0:T(8,128)(2,1)S(1)} %copy-done.1, f32[512]{0:T(512)S(1)} %copy-done.8, f32[1024]{0:T(1024)S(1)} %add_rsqrt_fusion, f32[1024]{0:T(1024)S(1)} %broadcast_multiply_fusion, pred[1024]{0:T(1024)(128)(4,1)S(1)} %broadcast_compare_fusion), kind=kLoop, calls=%fused_computation.2 | loop fusion | flops 3670016 | bytes 4205568 | tf_op jit(solution)/shard_map/convert_element_type | solution.py:76
  64.5 2.4 %copy.16 = bf16[1,1,1024,512]{3,2,1,0:T(8,128)(2,1)} copy(bf16[1,1,1024,512]{2,3,1,0:T(8,128)(2,1)} %bitcast.31) | data formatting | bytes 2097152
  66.9 0.0 copy-done.2
  66.9 1.9 %multiply_convert_fusion.1 = bf16[128,512]{1,0:T(8,128)(2,1)S(1)} fusion(f32[128,512]{1,0:T(8,128)S(1)} %fusion.15, bf16[1024,512]{1,0:T(8,128)(2,1)} %param.19, bf16[1024,512]{0,1:T(8,128)(2,1)S(1)} %copy-done.2, s32[1024]{0:T(1024)S(1)} %bitcast.40), kind=kOutput, calls=%fused_computation.26 | convolution fusion | flops 202047488 | bytes 1970176 | tf_op jit(solution)/shard_map/dot_general | solution.py:80
  68.9 0.3 fusion.33
  69.2 0.2 multiply_reduce_fusion.1
  69.4 0.0 copy-done.9
  69.4 0.8 %add_convert_fusion.1 = bf16[128,512]{1,0:T(8,128)(2,1)} fusion(f32[128,512]{1,0:T(8,128)S(1)} %get-tuple-element.13, f32[512]{0:T(512)S(1)} %copy-done.9, f32[128]{0:T(128)S(1)} %add_rsqrt_fusion.1, f32[128]{0:T(128)S(1)} %broadcast_multiply_fusion.1, bf16[8,16,512]{2,1,0:T(8,128)(2,1)S(1)} %copy-done.3), kind=kLoop, calls=%fused_computation.24 | loop fusion | flops 393216 | bytes 527360 | tf_op jit(solution)/shard_map/convert_element_type | solution.py:85
  (22 shorter events, 0.2 us)
Async XLA Ops:
  0.6 57.2 %copy-start = (bf16[512,512]{1,0:T(8,128)(2,1)S(1)}, bf16[512,512]{1,0:T(8,128)(2,1)}, u32[]{:S(2)}) copy-start(bf16[512,512]{1,0:T(8,128)(2,1)} %param.17) | copy-start | bytes 1572868
  0.6 22.8 %copy-start.3 = (bf16[8,16,512]{2,1,0:T(8,128)(2,1)S(1)}, bf16[8,16,512]{2,1,0:T(8,128)(2,1)}, u32[]{:S(2)}) copy-start(bf16[8,16,512]{2,1,0:T(8,128)(2,1)} %param.11) | copy-start | bytes 393220
  0.7 22.8 %copy-start.6 = (s32[1,1,1024]{2,1,0:T(1,128)S(1)}, s32[1,1,1024]{2,1,0:T(1,128)}, u32[]{:S(2)}) copy-start(s32[1,1,1024]{2,1,0:T(1,128)} %param.14) | copy-start | bytes 12292
  0.7 22.8 %copy-start.7 = (s32[1,1,1024]{2,1,0:T(1,128)S(1)}, s32[1,1,1024]{2,1,0:T(1,128)}, u32[]{:S(2)}) copy-start(s32[1,1,1024]{2,1,0:T(1,128)} %param.13) | copy-start | bytes 12292
  3.4 21.4 %copy-start.4 = (bf16[1,1,1024,512]{3,2,1,0:T(8,128)(2,1)S(1)}, bf16[1,1,1024,512]{3,2,1,0:T(8,128)(2,1)}, u32[]{:S(2)}) copy-start(bf16[1,1,1024,512]{3,2,1,0:T(8,128)(2,1)} %param.12) | copy-start | bytes 3145732
  4.1 22.0 %collective-permute-start.4 = (bf16[1,1,5,512]{3,2,1,0:T(8,128)(2,1)S(1)}, bf16[1,1,5,512]{3,2,1,0:T(8,128)(2,1)S(1)}, u32[]{:S(2)}, u32[]{:S(2)}) collective-permute-start(bf16[1,1,5,512]{3,2,1,0:T(8,128)(2,1)S(1)} %bitcast_select_fusion), channel_id=1, source_target_pairs={{0,16},{16,32},{32,48},{48,64},{64,80},{80,96},{96,112},{112,128},... | collective-permute-start | bytes 15368 | tf_op jit(solution)/shard_map/ppermute | solution.py:16
  6.0 20.1 %collective-permute-start.5 = (bf16[1,1,5,512]{3,2,1,0:T(8,128)(2,1)S(1)}, bf16[1,1,5,512]{3,2,1,0:T(8,128)(2,1)S(1)}, u32[]{:S(2)}, u32[]{:S(2)}) collective-permute-start(bf16[1,1,5,512]{3,2,1,0:T(8,128)(2,1)S(1)} %bitcast_select_fusion), channel_id=1, source_target_pairs={{16,0},{32,16},{48,32},{64,48},{80,64},{96,80},{112,96},{128,112},... | collective-permute-start | bytes 15368 | tf_op jit(solution)/shard_map/ppermute | solution.py:17
  12.6 21.8 %collective-permute-start = (bf16[1,16,512]{2,1,0:T(8,128)(2,1)S(1)}, bf16[1,16,512]{2,1,0:T(8,128)(2,1)S(1)}, u32[]{:S(2)}, u32[]{:S(2)}) collective-permute-start(bf16[1,16,512]{2,1,0:T(8,128)(2,1)S(1)} %get-tuple-element.8), channel_id=1, source_target_pairs={{0,16},{16,32},{32,48},{48,64},{64,80},{80,96},{96,112},{112,128},... | collective-permute-start | bytes 49160 | tf_op jit(solution)/shard_map/ppermute | solution.py:16
  14.6 19.9 %collective-permute-start.1 = (bf16[1,16,512]{2,1,0:T(8,128)(2,1)S(1)}, bf16[1,16,512]{2,1,0:T(8,128)(2,1)S(1)}, u32[]{:S(2)}, u32[]{:S(2)}) collective-permute-start(bf16[1,16,512]{2,1,0:T(8,128)(2,1)S(1)} %get-tuple-element.9), channel_id=1, source_target_pairs={{16,0},{32,16},{48,32},{64,48},{80,64},{96,80},{112,96},{128,112},... | collective-permute-start | bytes 49160 | tf_op jit(solution)/shard_map/ppermute | solution.py:17
  26.1 18.4 %collective-permute-start.6 = (bf16[3,1,5,512]{3,2,1,0:T(8,128)(2,1)S(1)}, bf16[3,1,5,512]{3,2,1,0:T(8,128)(2,1)S(1)}, u32[]{:S(2)}, u32[]{:S(2)}) collective-permute-start(bf16[3,1,5,512]{3,2,1,0:T(8,128)(2,1)S(1)} %pad_maximum_fusion.3), channel_id=1, source_target_pairs={{0,1},{1,2},{2,3},{3,4},{4,5},{5,6},{6,7},{7,8},{8,9},{9,10},{10,1... | collective-permute-start | bytes 46088 | tf_op jit(solution)/shard_map/ppermute | solution.py:16
  32.5 12.1 %collective-permute-start.7 = (bf16[3,1,5,512]{3,2,1,0:T(8,128)(2,1)S(1)}, bf16[3,1,5,512]{3,2,1,0:T(8,128)(2,1)S(1)}, u32[]{:S(2)}, u32[]{:S(2)}) collective-permute-start(bf16[3,1,5,512]{3,2,1,0:T(8,128)(2,1)S(1)} %pad_maximum_fusion.3), channel_id=1, source_target_pairs={{1,0},{2,1},{3,2},{4,3},{5,4},{6,5},{7,6},{8,7},{9,8},{10,9},{11,1... | collective-permute-start | bytes 46088 | tf_op jit(solution)/shard_map/ppermute | solution.py:17
  34.5 10.2 %collective-permute-start.2 = (bf16[10,1,512]{2,1,0:T(2,128)(2,1)S(1)}, bf16[10,1,512]{2,1,0:T(2,128)(2,1)S(1)}, u32[]{:S(2)}, u32[]{:S(2)}) collective-permute-start(bf16[10,1,512]{2,1,0:T(2,128)(2,1)S(1)} %get-tuple-element.6), channel_id=1, source_target_pairs={{0,1},{1,2},{2,3},{3,4},{4,5},{5,6},{6,7},{7,8},{8,9},{9,10},{10,1... | collective-permute-start | bytes 30728 | tf_op jit(solution)/shard_map/ppermute | solution.py:16
  42.6 9.9 %collective-permute-start.3 = (bf16[10,1,512]{2,1,0:T(2,128)(2,1)S(1)}, bf16[10,1,512]{2,1,0:T(2,128)(2,1)S(1)}, u32[]{:S(2)}, u32[]{:S(2)}) collective-permute-start(bf16[10,1,512]{2,1,0:T(2,128)(2,1)S(1)} %get-tuple-element.7), channel_id=1, source_target_pairs={{1,0},{2,1},{3,2},{4,3},{5,4},{6,5},{7,6},{8,7},{9,8},{10,9},{11,1... | collective-permute-start | bytes 30728 | tf_op jit(solution)/shard_map/ppermute | solution.py:17
  61.8 1.2 %copy-start.1 = (bf16[1,1,1024,512]{2,3,1,0:T(8,128)(2,1)S(1)}, bf16[1,1,1024,512]{2,3,1,0:T(8,128)(2,1)}, u32[]{:S(2)}) copy-start(bf16[1,1,1024,512]{2,3,1,0:T(8,128)(2,1)} %copy.15) | copy-start | bytes 3145732
  61.8 1.2 %copy-start.8 = (f32[512]{0:T(512)S(1)}, f32[512]{0:T(512)}, u32[]{:S(2)}) copy-start(f32[512]{0:T(512)} %param.18) | copy-start | bytes 6148
  64.5 2.4 %copy-start.2 = (bf16[1024,512]{0,1:T(8,128)(2,1)S(1)}, bf16[1024,512]{0,1:T(8,128)(2,1)}, u32[]{:S(2)}) copy-start(bf16[1024,512]{0,1:T(8,128)(2,1)} %add_convert_fusion) | copy-start | bytes 3145732
  64.5 4.3 %copy-start.5 = (bf16[512,512]{1,0:T(8,128)(2,1)S(1)}, bf16[512,512]{1,0:T(8,128)(2,1)}, u32[]{:S(2)}) copy-start(bf16[512,512]{1,0:T(8,128)(2,1)} %param.20) | copy-start | bytes 1572868
  66.9 2.5 %copy-start.9 = (f32[512]{0:T(512)S(1)}, f32[512]{0:T(512)}, u32[]{:S(2)}) copy-start(f32[512]{0:T(512)} %param.21) | copy-start | bytes 6148
where the time goes:
time: 70.7 us; the launch traced here: 70.2 us
  starting transfers between devices  34.5 us (49%)
  matrix products  11.9 us (17%)
  local copies, waits for them, and re-layouts  10.4 us (15%)
  waiting for transfers between devices  7.89 us (11%)
  other arithmetic  4.48 us (6%)
  between operations  0.97 us (1%)
    ppermute x4, starting transfers between devices, extended(): before = lax.ppermute(last, axis, up)  18.3 us
    ppermute x4, starting transfers between devices, extended(): after = lax.ppermute(leading, axis, down)  16.2 us
    ppermute x4, waiting for transfers between devices, extended(): after = lax.ppermute(leading, axis, down)  7.88 us
    gather x1, local copies, waits for them, and re-layouts, shards(): picked = jnp.take(sources, send_flat, axis=0)  5.08 us
    unnamed x22, local copies, waits for them, and re-layouts  4.65 us
    dot_general x1, matrix products, shards(): message = jnp.dot(hidden, edge_w2, preferred_element_type=jnp.float32)  3.97 us
    dot_general x1, matrix products, shards(): jnp.dot(landing, receiver_term, preferred_element_type=jnp.float32)  3.11 us
    dot_general x1, matrix products, shards(): jnp.dot(summed, node_w1[feature:], preferred_element_type=jnp.float32)  1.93 us
  transfers between devices with their start and end apart: 8, of which 1 were waited for; matrix products, arithmetic and copies ran while one was open for 8% of the time, Pallas kernels for 0%

commit v1 on v0

v1 whole, which is shorter than its diff:
```python
import functools

import jax
import jax.numpy as jnp
from jax import lax
from jax.experimental import pallas as pl
from jax.experimental.pallas import tpu as pltpu
from jax.sharding import PartitionSpec as P

eps = 1e-05
bf16 = jnp.bfloat16
f32 = jnp.float32
i32 = jnp.int32


def near_pairs(size):
    return [(i, i ^ 1) for i in range(size)]


def far_pairs(size):
    return [(i, (i + 1) % size if i % 2 else (i - 1) % size) for i in range(size)]


def dot(a, b):
    return jnp.dot(a, b, preferred_element_type=f32)


def silu(v):
    return v / (1.0 + jnp.exp(-v))


def normed(values, gain, keep=None):
    average = jnp.mean(values, -1, keepdims=True)
    centred = values - average
    variance = jnp.mean(centred * centred, -1, keepdims=True)
    scale = lax.rsqrt(variance + eps)
    if keep is not None:
        scale = jnp.where(keep, scale, 0.0)
    return centred * scale * gain


near1, far1, near2, far2, table_rows = 0, 24, 48, 80, 128


def pack_kernel(place_ref, nodes_ref, send_near, send_far, own_near, own_far):
    tile_x, tile_y = 8, 16
    last_row = (tile_x - 1) * tile_y
    odd_x = lax.rem(lax.axis_index("tx"), 2)
    odd_y = lax.rem(lax.axis_index("ty"), 2)
    count = nodes_ref.shape[0]
    row = lax.broadcasted_iota(i32, (80, count), 0)
    lane = lax.broadcasted_iota(i32, (80, count), 1)
    first = jnp.where(row < 24, 0, 24)
    within = row - first
    base = jnp.where(row < 24, last_row * (1 - odd_x), last_row * odd_x)
    border = base + jnp.where(
        within < tile_y, within, jnp.where(within == 21, 0, tile_y - 1)
    )
    side = row - jnp.where(row < 64, 48, 64)
    column = jnp.where(row < 64, (tile_y - 1) * (1 - odd_y), (tile_y - 1) * odd_y)
    edge_node = side * tile_y + column
    wanted = jnp.where(row < 48, border, edge_node)
    slot = jnp.where(row < 48, within - 16, side - 8)
    for k in range(5):
        wanted = jnp.where(slot == k, place_ref[k], wanted)
    pick = jnp.where(wanted == lane, 1.0, 0.0).astype(bf16)
    rows = dot(pick, nodes_ref[...]).astype(bf16)
    send_near[...] = rows[0:24]
    send_far[...] = rows[24:48]
    own_near[...] = rows[48:64]
    own_far[...] = rows[64:80]


def sender_slots(sender, place_ref):
    span = 18
    odd_x = lax.rem(lax.axis_index("tx"), 2)
    odd_y = lax.rem(lax.axis_index("ty"), 2)
    above, below = jnp.where(odd_x == 0, far1, near1), jnp.where(odd_x == 0, near1, far1)
    left, right = jnp.where(odd_y == 0, far2, near2), jnp.where(odd_y == 0, near2, far2)
    above_part, below_part = jnp.where(odd_x == 0, 24, 16), jnp.where(odd_x == 0, 16, 24)
    r = lax.div(sender, span)
    c = sender - r * span
    coarse = sender >= 180
    q = sender - 180
    w = lax.div(q, 5)
    k = q - w * 5
    wx = lax.div(w, 3)
    wy = w - wx * 3
    dx = jnp.where(coarse, wx, jnp.where(r == 0, 0, jnp.where(r == 9, 2, 1)))
    dy = jnp.where(coarse, wy, jnp.where(c == 0, 0, jnp.where(c == 17, 2, 1)))
    own_fine = (r - 1) * 16 + (c - 1)
    own_coarse = jnp.zeros_like(sender)
    for m in range(5):
        own_coarse = jnp.where(k == m, place_ref[m], own_coarse)
    mine = (dx == 1) & (dy == 1)
    own = jnp.where(mine, jnp.where(coarse, own_coarse, own_fine), -1)
    vertical = jnp.where(dx == 0, above, below) + jnp.where(coarse, 16 + k, c - 1)
    side = jnp.where(dy == 0, left, right)
    straight = side + jnp.where(coarse, 8 + k, r - 1)
    corner_part = jnp.where(dx == 0, above_part, below_part)
    corner = side + corner_part + jnp.where(coarse, k, jnp.where(dy == 0, 6, 5))
    away = jnp.where(dy == 1, vertical, jnp.where(dx == 1, straight, corner))
    return own, jnp.where(mine, -1, away)


def as_column(index, r):
    return jnp.broadcast_to(index[r : r + 1, :], (128, 128)).T


def one_hot(column, lane):
    return jnp.where(column == lane, 1.0, 0.0).astype(bf16)


def local_kernel(place_ref, nodes_ref, edges_ref, sender_ref, receiver_ref, w1_ref, node_w1_ref, pre_ref, node_pre_ref):
    feature = nodes_ref.shape[1]
    nodes = nodes_ref[...]
    own, _ = sender_slots(sender_ref[...], place_ref)
    receiver = receiver_ref[...]
    table = jnp.concatenate(
        [
            dot(nodes, w1_ref[feature : 2 * feature, :]).astype(bf16),
            dot(nodes, w1_ref[2 * feature :, :]).astype(bf16),
        ],
        axis=0,
    )
    node_pre_ref[...] = dot(nodes, node_w1_ref[0:feature, :])
    lane = lax.broadcasted_iota(i32, (128, 128), 1)
    for r in range(8):
        pick = jnp.concatenate(
            [one_hot(as_column(own, r), lane), one_hot(as_column(receiver, r), lane)], axis=1
        )
        rows = slice(r * 128, (r + 1) * 128)
        pre_ref[rows, :] = dot(edges_ref[rows, :], w1_ref[0:feature, :]) + dot(pick, table)


def finish_kernel(
    place_ref,
    near1_ref,
    far1_ref,
    near2_ref,
    far2_ref,
    pre_ref,
    node_pre_ref,
    nodes_ref,
    edges_ref,
    sender_ref,
    receiver_ref,
    w1_ref,
    w2_ref,
    edge_gain_ref,
    node_w1_ref,
    node_w2_ref,
    node_gain_ref,
    new_nodes_ref,
    new_edges_ref,
    updated_ref,
    table_ref,
    sems,
):
    feature = nodes_ref.shape[1]
    table_ref[near1:far1, :] = near1_ref[...]
    table_ref[far1:near2, :] = far1_ref[...]
    table_ref[near2:far2, :] = near2_ref[...]
    table_ref[far2 : far2 + 32, :] = far2_ref[...]
    table_ref[far2 + 32 :, :] = jnp.zeros((table_rows - far2 - 32, feature), bf16)
    table = dot(table_ref[...], w1_ref[feature : 2 * feature, :]).astype(bf16)
    _, away = sender_slots(sender_ref[...], place_ref)
    receiver = receiver_ref[...]
    lane = lax.broadcasted_iota(i32, (128, 128), 1)
    level = lax.broadcasted_iota(i32, (128, 128), 0)
    gain = edge_gain_ref[...]
    summed = jnp.zeros((128, feature), f32)
    copies = []
    for r in range(8):
        rows = slice(r * 128, (r + 1) * 128)
        pre = pre_ref[rows, :] + dot(one_hot(as_column(away, r), lane), table)
        hidden = silu(pre).astype(bf16)
        message = dot(hidden, w2_ref[...])
        live = as_column(receiver, r)[:, 0:1] < 128
        updated = (edges_ref[rows, :].astype(f32) + normed(message, gain, live)).astype(bf16)
        updated_ref[rows, :] = updated
        copy = pltpu.make_async_copy(updated_ref.at[rows, :], new_edges_ref.at[rows, :], sems.at[r])
        copy.start()
        copies.append(copy)
        landing = jnp.where(level == receiver[r : r + 1, :], 1.0, 0.0).astype(bf16)
        summed = summed + dot(landing, updated)
    hidden = silu(node_pre_ref[...] + dot(summed.astype(bf16), node_w1_ref[feature:, :])).astype(bf16)
    out = dot(hidden, node_w2_ref[...])
    new_nodes_ref[...] = (
        nodes_ref[...].astype(f32) + normed(out, node_gain_ref[...])
    ).astype(bf16)
    for copy in copies:
        copy.wait()


whole = pl.BlockSpec(memory_space=pltpu.VMEM)
scalars = pl.BlockSpec(memory_space=pltpu.SMEM)
anywhere = pl.BlockSpec(memory_space=pl.ANY)


def shards(sizes, nodes, edges, sender, receiver, place, w1, w2, edge_gain, node_w1, node_w2, node_gain):
    tile_x, tile_y, feature = nodes.shape
    size_x, size_y = sizes
    flat = nodes.reshape(tile_x * tile_y, feature)
    edge_flat = edges.reshape(-1, feature)
    send = sender.reshape(8, 128)
    recv = receiver.reshape(8, 128)
    row = jax.ShapeDtypeStruct((24, feature), bf16)
    col = jax.ShapeDtypeStruct((16, feature), bf16)
    send_near, send_far, own_near, own_far = pl.pallas_call(
        pack_kernel,
        out_shape=(row, row, col, col),
        in_specs=[scalars, whole],
        out_specs=(whole,) * 4,
        cost_estimate=pl.CostEstimate(flops=10_000_000_000, bytes_accessed=200_000, transcendentals=0),
        compiler_params=pltpu.CompilerParams(vmem_limit_bytes=4 << 20),
        name="pack",
    )(place, flat)
    got_far1 = lax.ppermute(send_far, "tx", far_pairs(size_x))
    got_near1 = lax.ppermute(send_near, "tx", near_pairs(size_x))
    pre, node_pre = pl.pallas_call(
        local_kernel,
        out_shape=(
            jax.ShapeDtypeStruct((1024, feature), f32),
            jax.ShapeDtypeStruct((128, feature), f32),
        ),
        in_specs=[scalars] + [whole] * 6,
        out_specs=(whole, whole),
        cost_estimate=pl.CostEstimate(flops=1_000_000_000, bytes_accessed=5_000_000, transcendentals=0),
        compiler_params=pltpu.CompilerParams(vmem_limit_bytes=24 << 20),
        name="local",
    )(place, flat, edge_flat, send, recv, w1, node_w1)
    tail = [got_near1[16:24], got_far1[16:24]]
    got_near2 = lax.ppermute(jnp.concatenate([own_near] + tail, 0), "ty", near_pairs(size_y))
    got_far2 = lax.ppermute(jnp.concatenate([own_far] + tail, 0), "ty", far_pairs(size_y))
    new_nodes, new_edges = pl.pallas_call(
        finish_kernel,
        out_shape=(
            jax.ShapeDtypeStruct((128, feature), bf16),
            jax.ShapeDtypeStruct((1024, feature), bf16),
        ),
        in_specs=[scalars] + [whole] * 16,
        out_specs=(whole, anywhere),
        scratch_shapes=[
            pltpu.VMEM((1024, feature), bf16),
            pltpu.VMEM((table_rows, feature), bf16),
            pltpu.SemaphoreType.DMA((8,)),
        ],
        cost_estimate=pl.CostEstimate(flops=1_100_000_000, bytes_accessed=6_000_000, transcendentals=600_000),
        compiler_params=pltpu.CompilerParams(vmem_limit_bytes=24 << 20),
        name="finish",
    )(
        place,
        got_near1,
        got_far1,
        got_near2,
        got_far2,
        pre,
        node_pre,
        flat,
        edge_flat,
        send,
        recv,
        w1,
        w2,
        edge_gain.reshape(1, feature),
        node_w1,
        node_w2,
        node_gain.reshape(1, feature),
    )
    return new_nodes.reshape(nodes.shape), new_edges.reshape(edges.shape)


def solution(mesh):
    placed = (
        P("tx", "ty", None),
        P("tx", "ty", None, None),
        P("tx", "ty", None),
        P("tx", "ty", None),
        P(("tx", "ty")),
        P(),
        P(),
        P(),
        P(),
        P(),
        P(),
    )
    sizes = (mesh.shape["tx"], mesh.shape["ty"])
    return jax.shard_map(
        functools.partial(shards, sizes),
        mesh=mesh,
        in_specs=placed,
        out_specs=(P("tx", "ty", None), P("tx", "ty", None, None)),
        check_vma=False,
    )
```

time: 70.7 us -> 38.6 us (0.55)
  the two profiles are of different devices: /device:TPU:134 before, /device:TPU:57 now
where the time goes in v1:
time: 38.6 us; the launch traced here: 38.4 us
  starting transfers between devices  20.6 us (53%)
  Pallas kernels  10.4 us (27%)
  waiting for transfers between devices  4.96 us (13%)
  local copies, waits for them, and re-layouts  1.61 us (4%)
  between operations  0.83 us (2%)
    ppermute x1, starting transfers between devices, shards(): lax.ppermute(jnp.concatenate([own_far] + tail, 0), 'ty', far_pairs(size_y))  12.9 us
    pallas_call x1, Pallas kernels, shards(): pl.pallas_call(finish_kernel, out_shape=(jax.ShapeDtypeStruct((128, featu...  7.89 us
    ppermute x1, waiting for transfers between devices, shards(): got_far1 = lax.ppermute(send_far, 'tx', far_pairs(size_x))  4.12 us
    ppermute x1, starting transfers between devices, shards(): got_far1 = lax.ppermute(send_far, 'tx', far_pairs(size_x))  3.1 us
    ppermute x1, starting transfers between devices, shards(): got_near1 = lax.ppermute(send_near, 'tx', near_pairs(size_x))  2.72 us
    ppermute x1, starting transfers between devices, shards(): lax.ppermute(jnp.concatenate([own_near] + tail, 0), 'ty', near_pairs(size...  1.92 us
    pallas_call x1, Pallas kernels, shards(): pl.pallas_call(local_kernel, out_shape=(jax.ShapeDtypeStruct((1024, featu...  1.82 us
    unnamed x26, local copies, waits for them, and re-layouts  1.6 us
  transfers between devices with their start and end apart: 4, of which 2 were waited for; matrix products, arithmetic and copies ran while one was open for 0% of the time, Pallas kernels for 5%

profile of v1, /device:TPU:57, one launch (start us, length us, event | category | flops | bytes accessed | tf_op | source)
XLA Modules:
  0.0 38.4 jit_solution(17432125010074406537)
XLA Ops:
  0.6 0.0 copy-start.3
  0.6 0.9 %copy-done.3 = bf16[8,16,512]{2,1,0:T(8,128)(2,1)S(1)} copy-done((bf16[8,16,512]{2,1,0:T(8,128)(2,1)S(1)}, bf16[8,16,512]{2,1,0:T(8,128)(2,1)}, u32[]{:S(2)}) %copy-start.3) | copy-done | bytes 131096
  1.5 0.0 copy-start.9
  1.5 0.7 %copy-done.9 = s32[5]{0:T(128)S(1)} copy-done((s32[5]{0:T(128)S(1)}, s32[5]{0:T(128)}, u32[]{:S(2)}) %copy-start.9) | copy-done | bytes 44
  2.2 0.0 copy-start
  2.2 0.0 copy-start.1
  2.2 0.0 copy-start.2
  2.2 0.0 copy-start.4
  2.2 0.0 copy-start.7
  2.2 0.0 copy-start.8
  2.2 0.0 copy-start.10
  2.2 0.7 %pack.1 = (bf16[24,512]{1,0:T(8,128)(2,1)S(1)}, bf16[24,512]{1,0:T(8,128)(2,1)S(1)}, bf16[16,512]{1,0:T(8,128)(2,1)S(1)}, bf16[16,512]{1,0:T(8,128)(2,1)S(1)}) custom-call(s32[5]{0:T(128)S(1)} %copy-done.9, bf16[128,512]{1,0:T(8,128)(2,1)S(1)} %bitcast.10), custom_call_target="tpu_custom_call" | custom-call | flops 10000000000 | bytes 200000 | tf_op jit(solution)/shard_map/pack/pallas_call | solution.py:210
  2.9 0.0 copy-start.5
  2.9 0.0 copy-start.6
  3.0 0.0 copy-start.11
  3.0 0.0 copy-start.12
  3.0 2.7 %collective-permute-start = (bf16[24,512]{1,0:T(8,128)(2,1)S(1)}, bf16[24,512]{1,0:T(8,128)(2,1)S(1)}, u32[]{:S(2)}, u32[]{:S(2)}) collective-permute-start(bf16[24,512]{1,0:T(8,128)(2,1)S(1)} %get-tuple-element.10), channel_id=1, source_target_pairs={{0,16},{16,0},{32,48},{48,32},{64,80},{80,64},{96,112},{112,96},{1... | collective-permute-start | bytes 73736 | tf_op jit(solution)/shard_map/ppermute | solution.py:220
  5.7 3.1 %collective-permute-start.1 = (bf16[24,512]{1,0:T(8,128)(2,1)S(1)}, bf16[24,512]{1,0:T(8,128)(2,1)S(1)}, u32[]{:S(2)}, u32[]{:S(2)}) collective-permute-start(bf16[24,512]{1,0:T(8,128)(2,1)S(1)} %get-tuple-element.11), channel_id=1, source_target_pairs={{0,496},{16,32},{32,16},{48,64},{64,48},{80,96},{96,80},{112,128},... | collective-permute-start | bytes 73736 | tf_op jit(solution)/shard_map/ppermute | solution.py:219
  8.8 0.0 collective-permute-done.near1_ref
  8.8 4.1 %collective-permute-done.1.far1_ref = bf16[24,512]{1,0:T(8,128)(2,1)S(1)} collective-permute-done((bf16[24,512]{1,0:T(8,128)(2,1)S(1)}, bf16[24,512]{1,0:T(8,128)(2,1)S(1)}, u32[]{:S(2)}, u32[]{:S(2)}) %collective-permute-start.1) | collective-permute-done | bytes 24608 | tf_op jit(solution)/shard_map/ppermute | solution.py:219
  13.0 12.9 %collective-permute-start.3 = (bf16[32,512]{1,0:T(8,128)(2,1)S(1)}, bf16[32,512]{1,0:T(8,128)(2,1)S(1)}, u32[]{:S(2)}, u32[]{:S(2)}) collective-permute-start(bf16[32,512]{1,0:T(8,128)(2,1)S(1)} %get-tuple-element.18), channel_id=1, source_target_pairs={{0,15},{1,2},{2,1},{3,4},{4,3},{5,6},{6,5},{7,8},{8,7},{9,10},{10,... | collective-permute-start | bytes 98312 | tf_op jit(solution)/shard_map/ppermute | solution.py:235
  25.8 1.9 %collective-permute-start.2 = (bf16[32,512]{1,0:T(8,128)(2,1)S(1)}, bf16[32,512]{1,0:T(8,128)(2,1)S(1)}, u32[]{:S(2)}, u32[]{:S(2)}) collective-permute-start(bf16[32,512]{1,0:T(8,128)(2,1)S(1)} %get-tuple-element.19), channel_id=1, source_target_pairs={{0,1},{1,0},{2,3},{3,2},{4,5},{5,4},{6,7},{7,6},{8,9},{9,8},{10,11... | collective-permute-start | bytes 98312 | tf_op jit(solution)/shard_map/ppermute | solution.py:234
  27.8 0.0 copy-done
  27.8 0.0 copy-done.1
  27.8 0.0 copy-done.2
  27.8 0.0 copy-done.4
  27.8 0.0 copy-done.7
  27.8 0.0 copy-done.8
  27.8 0.0 copy-done.10
  27.8 1.8 %local.1 = (f32[1024,512]{1,0:T(8,128)S(1)}, f32[128,512]{1,0:T(8,128)S(1)}) custom-call(s32[5]{0:T(128)S(1)} %copy-done.10, bf16[128,512]{1,0:T(8,128)(2,1)S(1)} %bitcast.11, bf16[1024,512]{1,0:T(8,128)(2,1)S(1)} %bitcast.8, s32[8,128]{1,0:T(8,128)S(1)} %bitcast.13, s32[8,128]{1,0:T(8,128)S(1)} %bitcast.15, bf16[1536,512]{1,0:T(8,128)(2,1)S(1)} %copy-done, ...), custom_call_target="tpu_custom_call" | custom-call | flops 1000000000 | bytes 5000000 | tf_op jit(solution)/shard_map/local/pallas_call | solution.py:221
  29.6 0.0 collective-permute-done.3.far2_ref
  29.7 0.8 %collective-permute-done.2.near2_ref = bf16[32,512]{1,0:T(8,128)(2,1)S(1)} collective-permute-done((bf16[32,512]{1,0:T(8,128)(2,1)S(1)}, bf16[32,512]{1,0:T(8,128)(2,1)S(1)}, u32[]{:S(2)}, u32[]{:S(2)}) %collective-permute-start.2) | collective-permute-done | bytes 32800 | tf_op jit(solution)/shard_map/ppermute | solution.py:234
  30.5 0.0 copy-done.5
  30.5 0.0 copy-done.6
  30.5 0.0 copy-done.11
  30.5 0.0 copy-done.12
  30.5 7.9 %finish.1 = (bf16[128,512]{1,0:T(8,128)(2,1)}, bf16[1024,512]{1,0:T(8,128)(2,1)}) custom-call(s32[5]{0:T(128)S(1)} %copy-done.10, bf16[24,512]{1,0:T(8,128)(2,1)S(1)} %collective-permute-done.near1_ref, bf16[24,512]{1,0:T(8,128)(2,1)S(1)} %collective-permute-done.1.far1_ref, bf16[32,512]{1,0:T(8,128)(2,1)S(1)} %collective-permute-done.2.near2_ref, ...), custom_call_target="tpu_custom_call" | custom-call | flops 1100000000 | bytes 6000000 | tf_op jit(solution)/shard_map/finish/pallas_call | solution.py:236
  (3 shorter events, 0.0 us)
Async XLA Ops:
  0.6 0.9 %copy-start.3 = (bf16[8,16,512]{2,1,0:T(8,128)(2,1)S(1)}, bf16[8,16,512]{2,1,0:T(8,128)(2,1)}, u32[]{:S(2)}) copy-start(bf16[8,16,512]{2,1,0:T(8,128)(2,1)} %param.11) | copy-start | bytes 393220
  1.5 0.7 %copy-start.9 = (s32[5]{0:T(128)S(1)}, s32[5]{0:T(128)}, u32[]{:S(2)}) copy-start(s32[5]{0:T(128)} %place_ref.5) | copy-start | bytes 64
  2.2 25.6 %copy-start = (bf16[1536,512]{1,0:T(8,128)(2,1)S(1)}, bf16[1536,512]{1,0:T(8,128)(2,1)}, u32[]{:S(2)}) copy-start(bf16[1536,512]{1,0:T(8,128)(2,1)} %w1_ref.3) | copy-start | bytes 4718596
  2.2 25.6 %copy-start.1 = (bf16[1,1,1024,512]{3,2,1,0:T(8,128)(2,1)S(1)}, bf16[1,1,1024,512]{3,2,1,0:T(8,128)(2,1)}, u32[]{:S(2)}) copy-start(bf16[1,1,1024,512]{3,2,1,0:T(8,128)(2,1)} %param.12) | copy-start | bytes 3145732
  2.2 25.6 %copy-start.2 = (bf16[1024,512]{1,0:T(8,128)(2,1)S(1)}, bf16[1024,512]{1,0:T(8,128)(2,1)}, u32[]{:S(2)}) copy-start(bf16[1024,512]{1,0:T(8,128)(2,1)} %node_w1_ref.3) | copy-start | bytes 3145732
  2.2 25.6 %copy-start.4 = (bf16[8,16,512]{2,1,0:T(8,128)(2,1)S(1)}, bf16[8,16,512]{2,1,0:T(8,128)(2,1)}, u32[]{:S(2)}) copy-start(bf16[8,16,512]{2,1,0:T(8,128)(2,1)} %param.11) | copy-start | bytes 393220
  2.2 25.6 %copy-start.7 = (s32[1,1,1024]{2,1,0:T(1,128)S(1)}, s32[1,1,1024]{2,1,0:T(1,128)}, u32[]{:S(2)}) copy-start(s32[1,1,1024]{2,1,0:T(1,128)} %param.13) | copy-start | bytes 12292
  2.2 25.6 %copy-start.8 = (s32[1,1,1024]{2,1,0:T(1,128)S(1)}, s32[1,1,1024]{2,1,0:T(1,128)}, u32[]{:S(2)}) copy-start(s32[1,1,1024]{2,1,0:T(1,128)} %param.14) | copy-start | bytes 12292
  2.2 25.6 %copy-start.10 = (s32[5]{0:T(128)S(1)}, s32[5]{0:T(128)}, u32[]{:S(2)}) copy-start(s32[5]{0:T(128)} %place_ref.5) | copy-start | bytes 64
  2.9 27.6 %copy-start.5 = (bf16[512,512]{1,0:T(8,128)(2,1)S(1)}, bf16[512,512]{1,0:T(8,128)(2,1)}, u32[]{:S(2)}) copy-start(bf16[512,512]{1,0:T(8,128)(2,1)} %w2_ref.1) | copy-start | bytes 1572868
  2.9 27.6 %copy-start.6 = (bf16[512,512]{1,0:T(8,128)(2,1)S(1)}, bf16[512,512]{1,0:T(8,128)(2,1)}, u32[]{:S(2)}) copy-start(bf16[512,512]{1,0:T(8,128)(2,1)} %node_w2_ref.1) | copy-start | bytes 1572868
  3.0 27.5 %copy-start.11 = (f32[512]{0:T(512)S(1)}, f32[512]{0:T(512)}, u32[]{:S(2)}) copy-start(f32[512]{0:T(512)} %param.18) | copy-start | bytes 6148
  3.0 27.5 %copy-start.12 = (f32[512]{0:T(512)S(1)}, f32[512]{0:T(512)}, u32[]{:S(2)}) copy-start(f32[512]{0:T(512)} %param.21) | copy-start | bytes 6148
  3.0 5.8 %collective-permute-start = (bf16[24,512]{1,0:T(8,128)(2,1)S(1)}, bf16[24,512]{1,0:T(8,128)(2,1)S(1)}, u32[]{:S(2)}, u32[]{:S(2)}) collective-permute-start(bf16[24,512]{1,0:T(8,128)(2,1)S(1)} %get-tuple-element.10), channel_id=1, source_target_pairs={{0,16},{16,0},{32,48},{48,32},{64,80},{80,64},{96,112},{112,96},{1... | collective-permute-start | bytes 73736 | tf_op jit(solution)/shard_map/ppermute | solution.py:220
  5.7 7.3 %collective-permute-start.1 = (bf16[24,512]{1,0:T(8,128)(2,1)S(1)}, bf16[24,512]{1,0:T(8,128)(2,1)S(1)}, u32[]{:S(2)}, u32[]{:S(2)}) collective-permute-start(bf16[24,512]{1,0:T(8,128)(2,1)S(1)} %get-tuple-element.11), channel_id=1, source_target_pairs={{0,496},{16,32},{32,16},{48,64},{64,48},{80,96},{96,80},{112,128},... | collective-permute-start | bytes 73736 | tf_op jit(solution)/shard_map/ppermute | solution.py:219
  13.0 16.7 %collective-permute-start.3 = (bf16[32,512]{1,0:T(8,128)(2,1)S(1)}, bf16[32,512]{1,0:T(8,128)(2,1)S(1)}, u32[]{:S(2)}, u32[]{:S(2)}) collective-permute-start(bf16[32,512]{1,0:T(8,128)(2,1)S(1)} %get-tuple-element.18), channel_id=1, source_target_pairs={{0,15},{1,2},{2,1},{3,4},{4,3},{5,6},{6,5},{7,8},{8,7},{9,10},{10,... | collective-permute-start | bytes 98312 | tf_op jit(solution)/shard_map/ppermute | solution.py:235
  25.8 4.7 %collective-permute-start.2 = (bf16[32,512]{1,0:T(8,128)(2,1)S(1)}, bf16[32,512]{1,0:T(8,128)(2,1)S(1)}, u32[]{:S(2)}, u32[]{:S(2)}) collective-permute-start(bf16[32,512]{1,0:T(8,128)(2,1)S(1)} %get-tuple-element.19), channel_id=1, source_target_pairs={{0,1},{1,0},{2,3},{3,2},{4,5},{5,4},{6,7},{7,6},{8,9},{9,8},{10,11... | collective-permute-start | bytes 98312 | tf_op jit(solution)/shard_map/ppermute | solution.py:234

commit v2 on v1

v2 whole, which is shorter than its diff:
```python
import functools

import jax
import jax.numpy as jnp
from jax import lax
from jax.experimental import pallas as pl
from jax.experimental.pallas import tpu as pltpu
from jax.sharding import PartitionSpec as P


eps = 1e-05
bf16 = jnp.bfloat16
f32 = jnp.float32
i32 = jnp.int32


def upward(size):
    return [(i, (i + 1) % size) for i in range(size)]


def downward(size):
    return [((i + 1) % size, i) for i in range(size)]


def near_pairs(size):
    return [(i, i ^ 1) for i in range(size)]


def far_pairs(size):
    return [(i, (i + 1) % size if i % 2 else (i - 1) % size) for i in range(size)]


def dot(a, b):
    return jnp.dot(a, b, preferred_element_type=f32)


def silu_of_half(u):
    return u + u * jnp.tanh(u)


def normed(values, gain, keep=None):
    average = jnp.mean(values, -1, keepdims=True)
    centred = values - average
    variance = jnp.mean(centred * centred, -1, keepdims=True)
    scale = lax.rsqrt(variance + eps)
    if keep is not None:
        scale = jnp.where(keep, scale, 0.0)
    return centred * scale * gain


near1, far1, from_left, from_right, table_rows = 0, 24, 48, 80, 128


def pack_kernel(place_hbm, nodes_hbm, send_near, send_far, own_last, own_first, place_rows, place_ref, nodes_ref, sems):
    copies = [
        pltpu.make_async_copy(nodes_hbm, nodes_ref, sems.at[0]),
        pltpu.make_async_copy(place_hbm, place_ref, sems.at[1]),
    ]
    for copy in copies:
        copy.start()
    tile_x, tile_y = 8, 16
    last_row = (tile_x - 1) * tile_y
    odd_x = lax.rem(lax.axis_index("tx"), 2)
    count = tile_x * tile_y
    row = lax.broadcasted_iota(i32, (80, count), 0)
    lane = lax.broadcasted_iota(i32, (80, count), 1)
    first = jnp.where(row < 24, 0, 24)
    within = row - first
    base = jnp.where(row < 24, last_row * (1 - odd_x), last_row * odd_x)
    border = base + jnp.where(
        within < tile_y, within, jnp.where(within == 21, 0, tile_y - 1)
    )
    side = row - jnp.where(row < 64, 48, 64)
    column = jnp.where(row < 64, tile_y - 1, 0)
    edge_node = side * tile_y + column
    wanted = jnp.where(row < 48, border, edge_node)
    slot = jnp.where(row < 48, within - 16, side - 8)
    for copy in copies:
        copy.wait()
    line = lax.broadcasted_iota(i32, (8, 128), 0)
    spread = jnp.zeros((8, 128), i32)
    for k in range(5):
        wanted = jnp.where(slot == k, place_ref[k], wanted)
        spread = jnp.where(line == k, place_ref[k], spread)
    place_rows[...] = spread
    pick = jnp.where(wanted == lane, 1.0, 0.0).astype(bf16)
    rows = dot(pick, nodes_ref[...]).astype(bf16)
    send_near[...] = rows[0:24]
    send_far[...] = rows[24:48]
    own_last[...] = rows[48:64]
    own_first[...] = rows[64:80]


def sender_slots(sender, place_ref):
    span = 18
    odd_x = lax.rem(lax.axis_index("tx"), 2)
    above, below = jnp.where(odd_x == 0, far1, near1), jnp.where(odd_x == 0, near1, far1)
    above_part, below_part = jnp.where(odd_x == 0, 24, 16), jnp.where(odd_x == 0, 16, 24)
    r = lax.div(sender, span)
    c = sender - r * span
    coarse = sender >= 180
    q = sender - 180
    w = lax.div(q, 5)
    k = q - w * 5
    wx = lax.div(w, 3)
    wy = w - wx * 3
    dx = jnp.where(coarse, wx, jnp.where(r == 0, 0, jnp.where(r == 9, 2, 1)))
    dy = jnp.where(coarse, wy, jnp.where(c == 0, 0, jnp.where(c == 17, 2, 1)))
    own_fine = (r - 1) * 16 + (c - 1)
    own_coarse = jnp.zeros_like(sender)
    for m in range(5):
        own_coarse = jnp.where(k == m, place_ref[m : m + 1, :], own_coarse)
    mine = (dx == 1) & (dy == 1)
    own = jnp.where(mine, jnp.where(coarse, own_coarse, own_fine), -1)
    vertical = jnp.where(dx == 0, above, below) + jnp.where(coarse, 16 + k, c - 1)
    side = jnp.where(dy == 0, from_left, from_right)
    straight = side + jnp.where(coarse, 8 + k, r - 1)
    corner_part = jnp.where(dx == 0, above_part, below_part)
    corner = side + corner_part + jnp.where(coarse, k, jnp.where(dy == 0, 6, 5))
    away = jnp.where(dy == 1, vertical, jnp.where(dx == 1, straight, corner))
    return own, jnp.where(mine, -1, away)


def as_column(index, r):
    return jnp.broadcast_to(index[r : r + 1, :], (128, 128)).T


def one_hot(column, lane):
    return jnp.where(column == lane, 1.0, 0.0).astype(bf16)


def local_kernel(place_ref, nodes_ref, edges_ref, sender_ref, receiver_ref, w1_ref, node_w1_ref, pre_ref, node_pre_ref, pick_ref, landing_ref):
    feature = nodes_ref.shape[1]
    nodes = nodes_ref[...]
    own, away = sender_slots(sender_ref[...], place_ref)
    receiver = receiver_ref[...]
    table = jnp.concatenate(
        [
            dot(nodes, w1_ref[feature : 2 * feature, :]).astype(bf16),
            dot(nodes, w1_ref[2 * feature :, :]).astype(bf16),
        ],
        axis=0,
    )
    node_pre_ref[...] = 0.5 * dot(nodes, node_w1_ref[0:feature, :])
    lane = lax.broadcasted_iota(i32, (128, 128), 1)
    for r in range(4):
        pick = jnp.concatenate(
            [
                jnp.concatenate([one_hot(as_column(own, 2 * r + t), lane) for t in range(2)], axis=0),
                jnp.concatenate([one_hot(as_column(receiver, 2 * r + t), lane) for t in range(2)], axis=0),
            ],
            axis=1,
        )
        rows = slice(r * 256, (r + 1) * 256)
        pre_ref[rows, :] = 0.5 * (dot(edges_ref[rows, :], w1_ref[0:feature, :]) + dot(pick, table))
    level = lax.broadcasted_iota(i32, (128, 128), 0)
    for r in range(8):
        rows = slice(r * 128, (r + 1) * 128)
        pick_ref[rows, :] = one_hot(as_column(away, r), lane)
        landing_ref[:, rows] = one_hot(receiver[r : r + 1, :], level)


def finish_kernel(
    near1_ref,
    far1_ref,
    from_left_ref,
    from_right_ref,
    pre_ref,
    node_pre_ref,
    nodes_ref,
    edges_ref,
    pick_ref,
    landing_ref,
    receiver_ref,
    w1_ref,
    w2_ref,
    edge_gain_ref,
    node_w1_ref,
    node_w2_ref,
    node_gain_ref,
    new_nodes_ref,
    new_edges_ref,
    updated_ref,
    table_ref,
    nodes_out_ref,
    sems,
):
    feature = nodes_ref.shape[1]
    table_ref[near1:far1, :] = near1_ref[...]
    table_ref[far1:from_left, :] = far1_ref[...]
    table_ref[from_left:from_right, :] = from_left_ref[...]
    table_ref[from_right : from_right + 32, :] = from_right_ref[...]
    table_ref[from_right + 32 :, :] = jnp.zeros((table_rows - from_right - 32, feature), bf16)
    table = dot(table_ref[...], w1_ref[feature : 2 * feature, :]).astype(bf16) * bf16(0.5)
    receiver = receiver_ref[...]
    live_count = jnp.sum(jnp.where(receiver < 128, 1, 0))
    gain = edge_gain_ref[...]
    summed = jnp.zeros((128, feature), f32)
    copies = []
    for r in range(2):
        rows = slice(r * 512, (r + 1) * 512)
        pre = pre_ref[rows, :] + dot(pick_ref[rows, :], table)
        hidden = silu_of_half(pre).astype(bf16)
        message = dot(hidden, w2_ref[...])
        live = lax.broadcasted_iota(i32, (512, 1), 0) < live_count - 512 * r
        updated = (edges_ref[rows, :].astype(f32) + normed(message, gain, live)).astype(bf16)
        updated_ref[rows, :] = updated
        copy = pltpu.make_async_copy(updated_ref.at[rows, :], new_edges_ref.at[rows, :], sems.at[r])
        copy.start()
        copies.append(copy)
    summed = dot(landing_ref[...], updated_ref[...])
    hidden = silu_of_half(
        node_pre_ref[...] + 0.5 * dot(summed.astype(bf16), node_w1_ref[feature:, :])
    ).astype(bf16)
    out = dot(hidden, node_w2_ref[...])
    for half in range(2):
        rows = slice(half * 64, half * 64 + 64)
        nodes_out_ref[rows, :] = (
            nodes_ref[rows, :].astype(f32) + normed(out[rows, :], node_gain_ref[...])
        ).astype(bf16)
        copy = pltpu.make_async_copy(nodes_out_ref.at[rows, :], new_nodes_ref.at[rows, :], sems.at[6 + half])
        copy.start()
        copies.append(copy)
    for copy in copies:
        copy.wait()


whole = pl.BlockSpec(memory_space=pltpu.VMEM)
scalars = pl.BlockSpec(memory_space=pltpu.SMEM)
anywhere = pl.BlockSpec(memory_space=pl.ANY)


def shards(sizes, *arrays):
    return layer(sizes, *arrays)


def layer(sizes, nodes, edges, sender, receiver, place, w1, w2, edge_gain, node_w1, node_w2, node_gain):
    tile_x, tile_y, feature = nodes.shape
    size_x, size_y = sizes
    flat = nodes.reshape(tile_x * tile_y, feature)
    edge_flat = edges.reshape(-1, feature)
    send = sender.reshape(8, 128)
    recv = receiver.reshape(8, 128)
    row = jax.ShapeDtypeStruct((24, feature), bf16)
    col = jax.ShapeDtypeStruct((16, feature), bf16)
    send_near, send_far, own_last, own_first, place_rows = pl.pallas_call(
        pack_kernel,
        out_shape=(row, row, col, col, jax.ShapeDtypeStruct((8, 128), i32)),
        in_specs=[pl.BlockSpec(memory_space=pltpu.HBM)] * 2,
        out_specs=(whole,) * 5,
        scratch_shapes=[
            pltpu.SMEM((5,), i32),
            pltpu.VMEM((128, feature), bf16),
            pltpu.SemaphoreType.DMA((2,)),
        ],
        cost_estimate=pl.CostEstimate(flops=10_000_000_000, bytes_accessed=200_000, transcendentals=0),
        compiler_params=pltpu.CompilerParams(vmem_limit_bytes=4 << 20),
        name="pack",
    )(
        pltpu.with_memory_space_constraint(place, pltpu.HBM),
        pltpu.with_memory_space_constraint(flat, pltpu.HBM),
    )
    got_far1 = lax.ppermute(send_far, "tx", far_pairs(size_x))
    got_near1 = lax.ppermute(send_near, "tx", near_pairs(size_x))
    pre, node_pre, pick, landing = pl.pallas_call(
        local_kernel,
        out_shape=(
            jax.ShapeDtypeStruct((1024, feature), f32),
            jax.ShapeDtypeStruct((128, feature), f32),
            jax.ShapeDtypeStruct((1024, table_rows), bf16),
            jax.ShapeDtypeStruct((128, 1024), bf16),
        ),
        in_specs=[whole] * 7,
        out_specs=(whole,) * 4,
        cost_estimate=pl.CostEstimate(flops=1_000_000_000, bytes_accessed=5_000_000, transcendentals=0),
        compiler_params=pltpu.CompilerParams(vmem_limit_bytes=24 << 20),
        name="local",
    )(place_rows, flat, edge_flat, send, recv, w1, node_w1)
    tail = [got_near1[16:24], got_far1[16:24]]
    got_from_left = lax.ppermute(jnp.concatenate([own_last] + tail, 0), "ty", upward(size_y))
    got_from_right = lax.ppermute(jnp.concatenate([own_first] + tail, 0), "ty", downward(size_y))
    new_nodes, new_edges = pl.pallas_call(
        finish_kernel,
        out_shape=(
            jax.ShapeDtypeStruct((128, feature), bf16),
            jax.ShapeDtypeStruct((1024, feature), bf16),
        ),
        in_specs=[whole] * 17,
        out_specs=(anywhere, anywhere),
        scratch_shapes=[
            pltpu.VMEM((1024, feature), bf16),
            pltpu.VMEM((table_rows, feature), bf16),
            pltpu.VMEM((128, feature), bf16),
            pltpu.SemaphoreType.DMA((8,)),
        ],
        cost_estimate=pl.CostEstimate(flops=1_100_000_000, bytes_accessed=6_000_000, transcendentals=600_000),
        compiler_params=pltpu.CompilerParams(vmem_limit_bytes=24 << 20),
        name="finish",
    )(
        got_near1,
        got_far1,
        got_from_left,
        got_from_right,
        pre,
        node_pre,
        flat,
        edge_flat,
        pick,
        landing,
        recv,
        w1,
        w2,
        edge_gain.reshape(1, feature),
        node_w1,
        node_w2,
        node_gain.reshape(1, feature),
    )
    return new_nodes.reshape(nodes.shape), new_edges.reshape(edges.shape)


def solution(mesh):
    placed = (
        P("tx", "ty", None),
        P("tx", "ty", None, None),
        P("tx", "ty", None),
        P("tx", "ty", None),
        P(("tx", "ty")),
        P(),
        P(),
        P(),
        P(),
        P(),
        P(),
    )
    sizes = (mesh.shape["tx"], mesh.shape["ty"])
    return jax.shard_map(
        functools.partial(shards, sizes),
        mesh=mesh,
        in_specs=placed,
        out_specs=(P("tx", "ty", None), P("tx", "ty", None, None)),
        check_vma=False,
    )
```

time: 38.6 us -> 37.3 us (0.966)
  waiting for transfers between devices: 4.96 us -> 9.71 us
  Pallas kernels: 10.4 us -> 5.85 us
  local copies, waits for them, and re-layouts: 1.61 us -> 0.05 us
    ppermute x4, waiting for transfers between devices: 4.96 us -> 9.71 us  [the longest x1 5.58 us: layer(): lax.ppermute(jnp.concatenate([own_last] + tail, 0), 'ty', upward(size_y))]
    pallas_call x3, Pallas kernels: 10.4 us -> 5.85 us  [the longest x1 3.31 us: layer(): pl.pallas_call(finish_kernel, out_shape=(jax.ShapeDtypeStruct((128, featu...]
    unnamed x26 -> x20, local copies, waits for them, and re-layouts: 1.6 us -> 0.05 us
  transfers between devices with their start and end apart: 4 -> 4, of which waited for: 2 -> 2; matrix products, arithmetic and copies ran while one was open for 0% -> 0% of each run, Pallas kernels for 5% -> 3%
where the time goes in v2:
time: 37.3 us; the launch traced here: 37.1 us
  starting transfers between devices  20.6 us (55%)
  waiting for transfers between devices  9.71 us (26%)
  Pallas kernels  5.85 us (16%)
  between operations  0.84 us (2%)
    ppermute x1, starting transfers between devices, layer(): lax.ppermute(jnp.concatenate([own_first] + tail, 0), 'ty', downward(size_y))  12.8 us
    ppermute x1, waiting for transfers between devices, layer(): lax.ppermute(jnp.concatenate([own_last] + tail, 0), 'ty', upward(size_y))  5.58 us
    ppermute x1, waiting for transfers between devices, layer(): got_far1 = lax.ppermute(send_far, 'tx', far_pairs(size_x))  4.13 us
    pallas_call x1, Pallas kernels, layer(): pl.pallas_call(finish_kernel, out_shape=(jax.ShapeDtypeStruct((128, featu...  3.31 us
    ppermute x1, starting transfers between devices, layer(): got_far1 = lax.ppermute(send_far, 'tx', far_pairs(size_x))  3.1 us
    ppermute x1, starting transfers between devices, layer(): got_near1 = lax.ppermute(send_near, 'tx', near_pairs(size_x))  2.72 us
    ppermute x1, starting transfers between devices, layer(): lax.ppermute(jnp.concatenate([own_last] + tail, 0), 'ty', upward(size_y))  1.92 us
    pallas_call x1, Pallas kernels, layer(): pl.pallas_call(local_kernel, out_shape=(jax.ShapeDtypeStruct((1024, featu...  1.29 us
  transfers between devices with their start and end apart: 4, of which 2 were waited for; matrix products, arithmetic and copies ran while one was open for 0% of the time, Pallas kernels for 3%

profile of v2, /device:TPU:57, one launch (start us, length us, event | category | flops | bytes accessed | tf_op | source)
XLA Modules:
  0.0 37.1 jit_solution(2371494969996007984)
XLA Ops:
  0.6 0.0 copy-start
  0.6 0.0 copy-start.1
  0.7 0.0 copy-start.2
  0.7 0.0 copy-start.3
  0.7 0.0 copy-start.6
  0.7 0.0 copy-start.7
  0.7 1.2 %pack.1 = (bf16[24,512]{1,0:T(8,128)(2,1)S(1)}, bf16[24,512]{1,0:T(8,128)(2,1)S(1)}, bf16[16,512]{1,0:T(8,128)(2,1)S(1)}, bf16[16,512]{1,0:T(8,128)(2,1)S(1)}, s32[8,128]{1,0:T(8,128)S(1)}) custom-call(s32[5]{0:T(128)} %place_hbm.1, bf16[128,512]{1,0:T(8,128)(2,1)} %bitcast.10), custom_call_target="tpu_custom_call" | custom-call | flops 10000000000 | bytes 200000 | tf_op jit(solution)/shard_map/pack/pallas_call | solution.py:246
  1.9 0.0 copy-start.4
  2.0 0.0 copy-start.5
  2.0 0.0 copy-start.8
  2.0 0.0 copy-start.9
  2.0 2.7 %collective-permute-start = (bf16[24,512]{1,0:T(8,128)(2,1)S(1)}, bf16[24,512]{1,0:T(8,128)(2,1)S(1)}, u32[]{:S(2)}, u32[]{:S(2)}) collective-permute-start(bf16[24,512]{1,0:T(8,128)(2,1)S(1)} %get-tuple-element.13), channel_id=1, source_target_pairs={{0,16},{16,0},{32,48},{48,32},{64,80},{80,64},{96,112},{112,96},{1... | collective-permute-start | bytes 73736 | tf_op jit(solution)/shard_map/ppermute | solution.py:264
  4.7 3.1 %collective-permute-start.1 = (bf16[24,512]{1,0:T(8,128)(2,1)S(1)}, bf16[24,512]{1,0:T(8,128)(2,1)S(1)}, u32[]{:S(2)}, u32[]{:S(2)}) collective-permute-start(bf16[24,512]{1,0:T(8,128)(2,1)S(1)} %get-tuple-element.14), channel_id=1, source_target_pairs={{0,496},{16,32},{32,16},{48,64},{64,48},{80,96},{96,80},{112,128},... | collective-permute-start | bytes 73736 | tf_op jit(solution)/shard_map/ppermute | solution.py:263
  7.8 0.0 collective-permute-done.near1_ref
  7.8 4.1 %collective-permute-done.1.far1_ref = bf16[24,512]{1,0:T(8,128)(2,1)S(1)} collective-permute-done((bf16[24,512]{1,0:T(8,128)(2,1)S(1)}, bf16[24,512]{1,0:T(8,128)(2,1)S(1)}, u32[]{:S(2)}, u32[]{:S(2)}) %collective-permute-start.1) | collective-permute-done | bytes 24608 | tf_op jit(solution)/shard_map/ppermute | solution.py:263
  12.0 12.8 %collective-permute-start.3 = (bf16[32,512]{1,0:T(8,128)(2,1)S(1)}, bf16[32,512]{1,0:T(8,128)(2,1)S(1)}, u32[]{:S(2)}, u32[]{:S(2)}) collective-permute-start(bf16[32,512]{1,0:T(8,128)(2,1)S(1)} %get-tuple-element.24), channel_id=1, source_target_pairs={{1,0},{2,1},{3,2},{4,3},{5,4},{6,5},{7,6},{8,7},{9,8},{10,9},{11,1... | collective-permute-start | bytes 98312 | tf_op jit(solution)/shard_map/ppermute | solution.py:281
  24.8 1.9 %collective-permute-start.2 = (bf16[32,512]{1,0:T(8,128)(2,1)S(1)}, bf16[32,512]{1,0:T(8,128)(2,1)S(1)}, u32[]{:S(2)}, u32[]{:S(2)}) collective-permute-start(bf16[32,512]{1,0:T(8,128)(2,1)S(1)} %get-tuple-element.25), channel_id=1, source_target_pairs={{0,1},{1,2},{2,3},{3,4},{4,5},{5,6},{6,7},{7,8},{8,9},{9,10},{10,1... | collective-permute-start | bytes 98312 | tf_op jit(solution)/shard_map/ppermute | solution.py:280
  26.8 0.0 copy-done
  26.8 0.0 copy-done.1
  26.8 0.0 copy-done.2
  26.8 0.0 copy-done.3
  26.8 0.0 copy-done.6
  26.8 0.0 copy-done.7
  26.8 1.3 %local.1 = (f32[1024,512]{1,0:T(8,128)S(1)}, f32[128,512]{1,0:T(8,128)S(1)}, bf16[1024,128]{1,0:T(8,128)(2,1)S(1)}, bf16[128,1024]{1,0:T(8,128)(2,1)S(1)}) custom-call(s32[8,128]{1,0:T(8,128)S(1)} %get-tuple-element.17.place_ref, bf16[128,512]{1,0:T(8,128)(2,1)S(1)} %bitcast.11, bf16[1024,512]{1,0:T(8,128)(2,1)S(1)} %bitcast.8, s32[8,128]{1,0:T(8,128)S(1)} %bitcast.15, ...), custom_call_target="tpu_custom_call" | custom-call | flops 1000000000 | bytes 5000000 | tf_op jit(solution)/shard_map/local/pallas_call | solution.py:265
  28.1 0.0 collective-permute-done.3.from_right_ref
  28.1 5.6 %collective-permute-done.2.from_left_ref = bf16[32,512]{1,0:T(8,128)(2,1)S(1)} collective-permute-done((bf16[32,512]{1,0:T(8,128)(2,1)S(1)}, bf16[32,512]{1,0:T(8,128)(2,1)S(1)}, u32[]{:S(2)}, u32[]{:S(2)}) %collective-permute-start.2) | collective-permute-done | bytes 32800 | tf_op jit(solution)/shard_map/ppermute | solution.py:280
  33.7 0.0 copy-done.4
  33.7 0.0 copy-done.5
  33.7 0.0 copy-done.8
  33.7 0.0 copy-done.9
  33.7 3.3 %finish.1 = (bf16[128,512]{1,0:T(8,128)(2,1)}, bf16[1024,512]{1,0:T(8,128)(2,1)}) custom-call(bf16[24,512]{1,0:T(8,128)(2,1)S(1)} %collective-permute-done.near1_ref, bf16[24,512]{1,0:T(8,128)(2,1)S(1)} %collective-permute-done.1.far1_ref, bf16[32,512]{1,0:T(8,128)(2,1)S(1)} %collective-permute-done.2.from_left_ref, ...), custom_call_target="tpu_custom_call" | custom-call | flops 1100000000 | bytes 6000000 | tf_op jit(solution)/shard_map/finish/pallas_call | solution.py:282
  (3 shorter events, 0.0 us)
Async XLA Ops:
  0.6 26.1 %copy-start = (bf16[1536,512]{1,0:T(8,128)(2,1)S(1)}, bf16[1536,512]{1,0:T(8,128)(2,1)}, u32[]{:S(2)}) copy-start(bf16[1536,512]{1,0:T(8,128)(2,1)} %w1_ref.3) | copy-start | bytes 4718596
  0.6 26.1 %copy-start.1 = (bf16[1,1,1024,512]{3,2,1,0:T(8,128)(2,1)S(1)}, bf16[1,1,1024,512]{3,2,1,0:T(8,128)(2,1)}, u32[]{:S(2)}) copy-start(bf16[1,1,1024,512]{3,2,1,0:T(8,128)(2,1)} %param.12) | copy-start | bytes 3145732
  0.7 26.1 %copy-start.2 = (bf16[1024,512]{1,0:T(8,128)(2,1)S(1)}, bf16[1024,512]{1,0:T(8,128)(2,1)}, u32[]{:S(2)}) copy-start(bf16[1024,512]{1,0:T(8,128)(2,1)} %node_w1_ref.3) | copy-start | bytes 3145732
  0.7 26.1 %copy-start.3 = (bf16[8,16,512]{2,1,0:T(8,128)(2,1)S(1)}, bf16[8,16,512]{2,1,0:T(8,128)(2,1)}, u32[]{:S(2)}) copy-start(bf16[8,16,512]{2,1,0:T(8,128)(2,1)} %param.11) | copy-start | bytes 393220
  0.7 26.1 %copy-start.6 = (s32[1,1,1024]{2,1,0:T(1,128)S(1)}, s32[1,1,1024]{2,1,0:T(1,128)}, u32[]{:S(2)}) copy-start(s32[1,1,1024]{2,1,0:T(1,128)} %param.14) | copy-start | bytes 12292
  0.7 26.1 %copy-start.7 = (s32[1,1,1024]{2,1,0:T(1,128)S(1)}, s32[1,1,1024]{2,1,0:T(1,128)}, u32[]{:S(2)}) copy-start(s32[1,1,1024]{2,1,0:T(1,128)} %param.13) | copy-start | bytes 12292
  1.9 31.8 %copy-start.4 = (bf16[512,512]{1,0:T(8,128)(2,1)S(1)}, bf16[512,512]{1,0:T(8,128)(2,1)}, u32[]{:S(2)}) copy-start(bf16[512,512]{1,0:T(8,128)(2,1)} %w2_ref.1) | copy-start | bytes 1572868
  2.0 31.8 %copy-start.5 = (bf16[512,512]{1,0:T(8,128)(2,1)S(1)}, bf16[512,512]{1,0:T(8,128)(2,1)}, u32[]{:S(2)}) copy-start(bf16[512,512]{1,0:T(8,128)(2,1)} %node_w2_ref.1) | copy-start | bytes 1572868
  2.0 31.8 %copy-start.8 = (f32[512]{0:T(512)S(1)}, f32[512]{0:T(512)}, u32[]{:S(2)}) copy-start(f32[512]{0:T(512)} %param.18) | copy-start | bytes 6148
  2.0 31.8 %copy-start.9 = (f32[512]{0:T(512)S(1)}, f32[512]{0:T(512)}, u32[]{:S(2)}) copy-start(f32[512]{0:T(512)} %param.21) | copy-start | bytes 6148
  2.0 5.8 %collective-permute-start = (bf16[24,512]{1,0:T(8,128)(2,1)S(1)}, bf16[24,512]{1,0:T(8,128)(2,1)S(1)}, u32[]{:S(2)}, u32[]{:S(2)}) collective-permute-start(bf16[24,512]{1,0:T(8,128)(2,1)S(1)} %get-tuple-element.13), channel_id=1, source_target_pairs={{0,16},{16,0},{32,48},{48,32},{64,80},{80,64},{96,112},{112,96},{1... | collective-permute-start | bytes 73736 | tf_op jit(solution)/shard_map/ppermute | solution.py:264
  4.7 7.3 %collective-permute-start.1 = (bf16[24,512]{1,0:T(8,128)(2,1)S(1)}, bf16[24,512]{1,0:T(8,128)(2,1)S(1)}, u32[]{:S(2)}, u32[]{:S(2)}) collective-permute-start(bf16[24,512]{1,0:T(8,128)(2,1)S(1)} %get-tuple-element.14), channel_id=1, source_target_pairs={{0,496},{16,32},{32,16},{48,64},{64,48},{80,96},{96,80},{112,128},... | collective-permute-start | bytes 73736 | tf_op jit(solution)/shard_map/ppermute | solution.py:263
  12.0 16.1 %collective-permute-start.3 = (bf16[32,512]{1,0:T(8,128)(2,1)S(1)}, bf16[32,512]{1,0:T(8,128)(2,1)S(1)}, u32[]{:S(2)}, u32[]{:S(2)}) collective-permute-start(bf16[32,512]{1,0:T(8,128)(2,1)S(1)} %get-tuple-element.24), channel_id=1, source_target_pairs={{1,0},{2,1},{3,2},{4,3},{5,4},{6,5},{7,6},{8,7},{9,8},{10,9},{11,1... | collective-permute-start | bytes 98312 | tf_op jit(solution)/shard_map/ppermute | solution.py:281
  24.8 8.9 %collective-permute-start.2 = (bf16[32,512]{1,0:T(8,128)(2,1)S(1)}, bf16[32,512]{1,0:T(8,128)(2,1)S(1)}, u32[]{:S(2)}, u32[]{:S(2)}) collective-permute-start(bf16[32,512]{1,0:T(8,128)(2,1)S(1)} %get-tuple-element.25), channel_id=1, source_target_pairs={{0,1},{1,2},{2,3},{3,4},{4,5},{5,6},{6,7},{7,8},{8,9},{9,10},{10,1... | collective-permute-start | bytes 98312 | tf_op jit(solution)/shard_map/ppermute | solution.py:280

commit v3 on v2

--- a/solution.py
+++ b/solution.py
@@ -20,10 +20,6 @@
 
 def downward(size):
     return [((i + 1) % size, i) for i in range(size)]
-
-
-def near_pairs(size):
-    return [(i, i ^ 1) for i in range(size)]
 
 
 def far_pairs(size):
@@ -129,7 +125,7 @@
     return jnp.where(column == lane, 1.0, 0.0).astype(bf16)
 
 
-def local_kernel(place_ref, nodes_ref, edges_ref, sender_ref, receiver_ref, w1_ref, node_w1_ref, pre_ref, node_pre_ref, pick_ref, landing_ref):
+def local_kernel(place_ref, nodes_ref, edges_ref, sender_ref, receiver_ref, w1_ref, pre_ref, pick_ref, landing_ref):
     feature = nodes_ref.shape[1]
     nodes = nodes_ref[...]
     own, away = sender_slots(sender_ref[...], place_ref)
@@ -141,7 +137,6 @@
         ],
         axis=0,
     )
-    node_pre_ref[...] = 0.5 * dot(nodes, node_w1_ref[0:feature, :])
     lane = lax.broadcasted_iota(i32, (128, 128), 1)
     for r in range(4):
         pick = jnp.concatenate(
@@ -166,7 +161,6 @@
     from_left_ref,
     from_right_ref,
     pre_ref,
-    node_pre_ref,
     nodes_ref,
     edges_ref,
     pick_ref,
@@ -175,18 +169,29 @@
     w1_ref,
     w2_ref,
     edge_gain_ref,
-    node_w1_ref,
-    node_w2_ref,
+    node_w1_hbm,
+    node_w2_hbm,
     node_gain_ref,
     new_nodes_ref,
     new_edges_ref,
     updated_ref,
     table_ref,
     nodes_out_ref,
+    node_w1_ref,
+    node_w2_ref,
     sems,
+    weight_sems,
 ):
     feature = nodes_ref.shape[1]
-    table_ref[near1:far1, :] = near1_ref[...]
+    weights = [
+        pltpu.make_async_copy(node_w1_hbm, node_w1_ref, weight_sems.at[0]),
+        pltpu.make_async_copy(node_w2_hbm, node_w2_ref, weight_sems.at[1]),
+    ]
+    for copy in weights:
+        copy.start()
+    table_ref[near1:far1, :] = jnp.where(
+        lax.rem(lax.axis_index("tx"), 2) == 0, near1_ref[24:48, :], near1_ref[0:24, :]
+    )
     table_ref[far1:from_left, :] = far1_ref[...]
     table_ref[from_left:from_right, :] = from_left_ref[...]
     table_ref[from_right : from_right + 32, :] = from_right_ref[...]
@@ -209,8 +214,14 @@
         copy.start()
         copies.append(copy)
     summed = dot(landing_ref[...], updated_ref[...])
+    for copy in weights:
+        copy.wait()
     hidden = silu_of_half(
-        node_pre_ref[...] + 0.5 * dot(summed.astype(bf16), node_w1_ref[feature:, :])
+        0.5
+        * (
+            dot(nodes_ref[...], node_w1_ref[0:feature, :])
+            + dot(summed.astype(bf16), node_w1_ref[feature:, :])
+        )
     ).astype(bf16)
     out = dot(hidden, node_w2_ref[...])
     for half in range(2):
@@ -228,6 +239,7 @@
 whole = pl.BlockSpec(memory_space=pltpu.VMEM)
 scalars = pl.BlockSpec(memory_space=pltpu.SMEM)
 anywhere = pl.BlockSpec(memory_space=pl.ANY)
+in_hbm = pl.BlockSpec(memory_space=pltpu.HBM)
 
 
 def shards(sizes, *arrays):
@@ -235,6 +247,8 @@
 
 
 def layer(sizes, nodes, edges, sender, receiver, place, w1, w2, edge_gain, node_w1, node_w2, node_gain):
+    node_w1 = pltpu.with_memory_space_constraint(node_w1, pltpu.HBM)
+    node_w2 = pltpu.with_memory_space_constraint(node_w2, pltpu.HBM)
     tile_x, tile_y, feature = nodes.shape
     size_x, size_y = sizes
     flat = nodes.reshape(tile_x * tile_y, feature)
@@ -261,22 +275,24 @@
         pltpu.with_memory_space_constraint(flat, pltpu.HBM),
     )
     got_far1 = lax.ppermute(send_far, "tx", far_pairs(size_x))
-    got_near1 = lax.ppermute(send_near, "tx", near_pairs(size_x))
-    pre, node_pre, pick, landing = pl.pallas_call(
+    pair = lax.all_gather(
+        send_near, "tx", axis_index_groups=[[i, i + 1] for i in range(0, size_x, 2)], tiled=True
+    )
+    tails = jnp.where(lax.axis_index("tx") % 2 == 0, pair[40:48], pair[16:24])
+    pre, pick, landing = pl.pallas_call(
         local_kernel,
         out_shape=(
             jax.ShapeDtypeStruct((1024, feature), f32),
-            jax.ShapeDtypeStruct((128, feature), f32),
             jax.ShapeDtypeStruct((1024, table_rows), bf16),
             jax.ShapeDtypeStruct((128, 1024), bf16),
         ),
-        in_specs=[whole] * 7,
-        out_specs=(whole,) * 4,
+        in_specs=[whole] * 6,
+        out_specs=(whole,) * 3,
         cost_estimate=pl.CostEstimate(flops=1_000_000_000, bytes_accessed=5_000_000, transcendentals=0),
         compiler_params=pltpu.CompilerParams(vmem_limit_bytes=24 << 20),
         name="local",
-    )(place_rows, flat, edge_flat, send, recv, w1, node_w1)
-    tail = [got_near1[16:24], got_far1[16:24]]
+    )(place_rows, flat, edge_flat, send, recv, w1)
+    tail = [tails, got_far1[16:24]]
     got_from_left = lax.ppermute(jnp.concatenate([own_last] + tail, 0), "ty", upward(size_y))
     got_from_right = lax.ppermute(jnp.concatenate([own_first] + tail, 0), "ty", downward(size_y))
     new_nodes, new_edges = pl.pallas_call(
@@ -285,24 +301,26 @@
             jax.ShapeDtypeStruct((128, feature), bf16),
             jax.ShapeDtypeStruct((1024, feature), bf16),
         ),
-        in_specs=[whole] * 17,
+        in_specs=[whole] * 13 + [in_hbm] * 2 + [whole],
         out_specs=(anywhere, anywhere),
         scratch_shapes=[
             pltpu.VMEM((1024, feature), bf16),
             pltpu.VMEM((table_rows, feature), bf16),
             pltpu.VMEM((128, feature), bf16),
+            pltpu.VMEM((2 * feature, feature), bf16),
+            pltpu.VMEM((feature, feature), bf16),
             pltpu.SemaphoreType.DMA((8,)),
+            pltpu.SemaphoreType.DMA((2,)),
         ],
         cost_estimate=pl.CostEstimate(flops=1_100_000_000, bytes_accessed=6_000_000, transcendentals=600_000),
         compiler_params=pltpu.CompilerParams(vmem_limit_bytes=24 << 20),
         name="finish",
     )(
-        got_near1,
+        pair,
         got_far1,
         got_from_left,
         got_from_right,
         pre,
-        node_pre,
         flat,
         edge_flat,
         pick,

time: 37.3 us -> 37.3 us (level)
  the two profiles are of different devices: /device:TPU:57 before, /device:TPU:1 now
where the time goes in v3:
time: 37.3 us; the launch traced here: 37.1 us
  starting transfers between devices  18 us (48%)
  Pallas kernels  7.03 us (19%)
  blocking collectives  5.67 us (15%)
  waiting for transfers between devices  5.59 us (15%)
  between operations  0.81 us (2%)
    ppermute x1, starting transfers between devices, layer(): lax.ppermute(jnp.concatenate([own_first] + tail, 0), 'ty', downward(size_y))  11.3 us
    all_gather x1, blocking collectives, layer(): lax.all_gather(send_near, 'tx', axis_index_groups=[[i, i + 1] for i in ra...  5.67 us
    ppermute x1, waiting for transfers between devices, layer(): lax.ppermute(jnp.concatenate([own_last] + tail, 0), 'ty', upward(size_y))  5.59 us
    ppermute x1, starting transfers between devices, layer(): got_far1 = lax.ppermute(send_far, 'tx', far_pairs(size_x))  4.72 us
    pallas_call x1, Pallas kernels, layer(): pl.pallas_call(finish_kernel, out_shape=(jax.ShapeDtypeStruct((128, featu...  4.5 us
    ppermute x1, starting transfers between devices, layer(): lax.ppermute(jnp.concatenate([own_last] + tail, 0), 'ty', upward(size_y))  1.92 us
    pallas_call x1, Pallas kernels, layer(): pl.pallas_call(local_kernel, out_shape=(jax.ShapeDtypeStruct((1024, featu...  1.29 us
    pallas_call x1, Pallas kernels, layer(): pl.pallas_call(pack_kernel, out_shape=(row, row, col, col, jax.ShapeDtype...  1.24 us
  transfers between devices with their start and end apart: 3, of which 1 were waited for; matrix products, arithmetic and copies ran while one was open for 0% of the time, Pallas kernels for 3%

profile of v3, /device:TPU:1, one launch (start us, length us, event | category | flops | bytes accessed | tf_op | source)
XLA Modules:
  0.0 37.1 jit_solution(15577240192134835647)
XLA Ops:
  0.6 0.0 copy-start
  0.6 0.0 copy-start.1
  0.7 0.0 copy-start.3
  0.7 0.0 copy-start.4
  0.7 0.0 copy-start.7
  0.7 1.2 %pack.1 = (bf16[24,512]{1,0:T(8,128)(2,1)S(1)}, bf16[24,512]{1,0:T(8,128)(2,1)S(1)}, bf16[16,512]{1,0:T(8,128)(2,1)S(1)}, bf16[16,512]{1,0:T(8,128)(2,1)S(1)}, s32[8,128]{1,0:T(8,128)S(1)}) custom-call(s32[5]{0:T(128)} %place_hbm.1, bf16[128,512]{1,0:T(8,128)(2,1)} %bitcast.10), custom_call_target="tpu_custom_call" | custom-call | flops 10000000000 | bytes 200000 | tf_op jit(solution)/shard_map/pack/pallas_call | solution.py:260
  1.9 0.0 copy-start.2
  1.9 0.0 copy-start.5
  2.0 0.0 copy-start.6
  2.0 4.7 %collective-permute-start = (bf16[24,512]{1,0:T(8,128)(2,1)S(1)}, bf16[24,512]{1,0:T(8,128)(2,1)S(1)}, u32[]{:S(2)}, u32[]{:S(2)}) collective-permute-start(bf16[24,512]{1,0:T(8,128)(2,1)S(1)} %get-tuple-element.13), channel_id=1, source_target_pairs={{0,496},{16,32},{32,16},{48,64},{64,48},{80,96},{96,80},{112,128},... | collective-permute-start | bytes 73736 | tf_op jit(solution)/shard_map/ppermute | solution.py:277
  6.7 5.7 %all_gather.3.near1_ref = bf16[48,512]{1,0:T(8,128)(2,1)S(1)} all-gather(bf16[24,512]{1,0:T(8,128)(2,1)S(1)} %get-tuple-element.12), channel_id=1, replica_groups={{0,16},{32,48},{64,80},{96,112},{128,144},{160,176},{192,208},{224,240}..., dimensions={0}, use_global_device_ids=true | all-gather | bytes 73728 | tf_op jit(solution)/shard_map/all_gather | solution.py:278
  12.4 0.0 collective-permute-done.far1_ref
  12.4 11.3 %collective-permute-start.2 = (bf16[32,512]{1,0:T(8,128)(2,1)S(1)}, bf16[32,512]{1,0:T(8,128)(2,1)S(1)}, u32[]{:S(2)}, u32[]{:S(2)}) collective-permute-start(bf16[32,512]{1,0:T(8,128)(2,1)S(1)} %get-tuple-element.22), channel_id=1, source_target_pairs={{1,0},{2,1},{3,2},{4,3},{5,4},{6,5},{7,6},{8,7},{9,8},{10,9},{11,1... | collective-permute-start | bytes 98312 | tf_op jit(solution)/shard_map/ppermute | solution.py:297
  23.7 1.9 %collective-permute-start.1 = (bf16[32,512]{1,0:T(8,128)(2,1)S(1)}, bf16[32,512]{1,0:T(8,128)(2,1)S(1)}, u32[]{:S(2)}, u32[]{:S(2)}) collective-permute-start(bf16[32,512]{1,0:T(8,128)(2,1)S(1)} %get-tuple-element.23), channel_id=1, source_target_pairs={{0,1},{1,2},{2,3},{3,4},{4,5},{5,6},{6,7},{7,8},{8,9},{9,10},{10,1... | collective-permute-start | bytes 98312 | tf_op jit(solution)/shard_map/ppermute | solution.py:296
  25.6 0.0 copy-done
  25.7 0.0 copy-done.1
  25.7 0.0 copy-done.3
  25.7 0.0 copy-done.4
  25.7 0.0 copy-done.7
  25.7 1.3 %local.1 = (f32[1024,512]{1,0:T(8,128)S(1)}, bf16[1024,128]{1,0:T(8,128)(2,1)S(1)}, bf16[128,1024]{1,0:T(8,128)(2,1)S(1)}) custom-call(s32[8,128]{1,0:T(8,128)S(1)} %get-tuple-element.16.place_ref, bf16[128,512]{1,0:T(8,128)(2,1)S(1)} %bitcast.11, bf16[1024,512]{1,0:T(8,128)(2,1)S(1)} %bitcast.8, s32[8,128]{1,0:T(8,128)S(1)} %bitcast.17, ...), custom_call_target="tpu_custom_call" | custom-call | flops 1000000000 | bytes 5000000 | tf_op jit(solution)/shard_map/local/pallas_call | solution.py:282
  27.0 0.0 collective-permute-done.2.from_right_ref
  27.0 5.6 %collective-permute-done.1.from_left_ref = bf16[32,512]{1,0:T(8,128)(2,1)S(1)} collective-permute-done((bf16[32,512]{1,0:T(8,128)(2,1)S(1)}, bf16[32,512]{1,0:T(8,128)(2,1)S(1)}, u32[]{:S(2)}, u32[]{:S(2)}) %collective-permute-start.1) | collective-permute-done | bytes 32800 | tf_op jit(solution)/shard_map/ppermute | solution.py:296
  32.6 0.0 copy-done.2
  32.6 0.0 copy-done.5
  32.6 0.0 copy-done.6
  32.6 4.5 %finish.1 = (bf16[128,512]{1,0:T(8,128)(2,1)}, bf16[1024,512]{1,0:T(8,128)(2,1)}) custom-call(bf16[48,512]{1,0:T(8,128)(2,1)S(1)} %all_gather.3.near1_ref, bf16[24,512]{1,0:T(8,128)(2,1)S(1)} %collective-permute-done.far1_ref, bf16[32,512]{1,0:T(8,128)(2,1)S(1)} %collective-permute-done.1.from_left_ref, ...), custom_call_target="tpu_custom_call" | custom-call | flops 1100000000 | bytes 6000000 | tf_op jit(solution)/shard_map/finish/pallas_call | solution.py:298
  (3 shorter events, 0.0 us)
Async XLA Ops:
  0.6 25.0 %copy-start = (bf16[1536,512]{1,0:T(8,128)(2,1)S(1)}, bf16[1536,512]{1,0:T(8,128)(2,1)}, u32[]{:S(2)}) copy-start(bf16[1536,512]{1,0:T(8,128)(2,1)} %w1_ref.3) | copy-start | bytes 4718596
  0.6 25.0 %copy-start.1 = (bf16[1,1,1024,512]{3,2,1,0:T(8,128)(2,1)S(1)}, bf16[1,1,1024,512]{3,2,1,0:T(8,128)(2,1)}, u32[]{:S(2)}) copy-start(bf16[1,1,1024,512]{3,2,1,0:T(8,128)(2,1)} %param.12) | copy-start | bytes 3145732
  0.7 25.0 %copy-start.3 = (bf16[8,16,512]{2,1,0:T(8,128)(2,1)S(1)}, bf16[8,16,512]{2,1,0:T(8,128)(2,1)}, u32[]{:S(2)}) copy-start(bf16[8,16,512]{2,1,0:T(8,128)(2,1)} %param.11) | copy-start | bytes 393220
  0.7 25.0 %copy-start.4 = (s32[1,1,1024]{2,1,0:T(1,128)S(1)}, s32[1,1,1024]{2,1,0:T(1,128)}, u32[]{:S(2)}) copy-start(s32[1,1,1024]{2,1,0:T(1,128)} %param.14) | copy-start | bytes 12292
  0.7 25.0 %copy-start.7 = (s32[1,1,1024]{2,1,0:T(1,128)S(1)}, s32[1,1,1024]{2,1,0:T(1,128)}, u32[]{:S(2)}) copy-start(s32[1,1,1024]{2,1,0:T(1,128)} %param.13) | copy-start | bytes 12292
  1.9 30.7 %copy-start.2 = (bf16[512,512]{1,0:T(8,128)(2,1)S(1)}, bf16[512,512]{1,0:T(8,128)(2,1)}, u32[]{:S(2)}) copy-start(bf16[512,512]{1,0:T(8,128)(2,1)} %w2_ref.1) | copy-start | bytes 1572868
  1.9 30.7 %copy-start.5 = (f32[512]{0:T(512)S(1)}, f32[512]{0:T(512)}, u32[]{:S(2)}) copy-start(f32[512]{0:T(512)} %param.18) | copy-start | bytes 6148
  2.0 30.7 %copy-start.6 = (f32[512]{0:T(512)S(1)}, f32[512]{0:T(512)}, u32[]{:S(2)}) copy-start(f32[512]{0:T(512)} %param.21) | copy-start | bytes 6148
  2.0 10.4 %collective-permute-start = (bf16[24,512]{1,0:T(8,128)(2,1)S(1)}, bf16[24,512]{1,0:T(8,128)(2,1)S(1)}, u32[]{:S(2)}, u32[]{:S(2)}) collective-permute-start(bf16[24,512]{1,0:T(8,128)(2,1)S(1)} %get-tuple-element.13), channel_id=1, source_target_pairs={{0,496},{16,32},{32,16},{48,64},{64,48},{80,96},{96,80},{112,128},... | collective-permute-start | bytes 73736 | tf_op jit(solution)/shard_map/ppermute | solution.py:277
  12.4 14.6 %collective-permute-start.2 = (bf16[32,512]{1,0:T(8,128)(2,1)S(1)}, bf16[32,512]{1,0:T(8,128)(2,1)S(1)}, u32[]{:S(2)}, u32[]{:S(2)}) collective-permute-start(bf16[32,512]{1,0:T(8,128)(2,1)S(1)} %get-tuple-element.22), channel_id=1, source_target_pairs={{1,0},{2,1},{3,2},{4,3},{5,4},{6,5},{7,6},{8,7},{9,8},{10,9},{11,1... | collective-permute-start | bytes 98312 | tf_op jit(solution)/shard_map/ppermute | solution.py:297
  23.7 8.9 %collective-permute-start.1 = (bf16[32,512]{1,0:T(8,128)(2,1)S(1)}, bf16[32,512]{1,0:T(8,128)(2,1)S(1)}, u32[]{:S(2)}, u32[]{:S(2)}) collective-permute-start(bf16[32,512]{1,0:T(8,128)(2,1)S(1)} %get-tuple-element.23), channel_id=1, source_target_pairs={{0,1},{1,2},{2,3},{3,4},{4,5},{5,6},{6,7},{7,8},{8,9},{9,10},{10,1... | collective-permute-start | bytes 98312 | tf_op jit(solution)/shard_map/ppermute | solution.py:296

commit v4 on v3

--- a/solution.py
+++ b/solution.py
@@ -48,10 +48,12 @@
 
 
 def pack_kernel(place_hbm, nodes_hbm, send_near, send_far, own_last, own_first, place_rows, place_ref, nodes_ref, sems):
-    copies = [
-        pltpu.make_async_copy(nodes_hbm, nodes_ref, sems.at[0]),
-        pltpu.make_async_copy(place_hbm, place_ref, sems.at[1]),
-    ]
+    copies = [pltpu.make_async_copy(place_hbm, place_ref, sems.at[4])]
+    for n in range(4):
+        some = slice(n * 32, (n + 1) * 32)
+        copies.append(
+            pltpu.make_async_copy(nodes_hbm.at[some, :], nodes_ref.at[some, :], sems.at[n])
+        )
     for copy in copies:
         copy.start()
     tile_x, tile_y = 8, 16
@@ -184,7 +186,8 @@
 ):
     feature = nodes_ref.shape[1]
     weights = [
-        pltpu.make_async_copy(node_w1_hbm, node_w1_ref, weight_sems.at[0]),
+        pltpu.make_async_copy(node_w1_hbm.at[0:feature, :], node_w1_ref.at[0:feature, :], weight_sems.at[0]),
+        pltpu.make_async_copy(node_w1_hbm.at[feature:, :], node_w1_ref.at[feature:, :], weight_sems.at[2]),
         pltpu.make_async_copy(node_w2_hbm, node_w2_ref, weight_sems.at[1]),
     ]
     for copy in weights:
@@ -265,7 +268,7 @@
         scratch_shapes=[
             pltpu.SMEM((5,), i32),
             pltpu.VMEM((128, feature), bf16),
-            pltpu.SemaphoreType.DMA((2,)),
+            pltpu.SemaphoreType.DMA((5,)),
         ],
         cost_estimate=pl.CostEstimate(flops=10_000_000_000, bytes_accessed=200_000, transcendentals=0),
         compiler_params=pltpu.CompilerParams(vmem_limit_bytes=4 << 20),
@@ -310,7 +313,7 @@
             pltpu.VMEM((2 * feature, feature), bf16),
             pltpu.VMEM((feature, feature), bf16),
             pltpu.SemaphoreType.DMA((8,)),
-            pltpu.SemaphoreType.DMA((2,)),
+            pltpu.SemaphoreType.DMA((3,)),
         ],
         cost_estimate=pl.CostEstimate(flops=1_100_000_000, bytes_accessed=6_000_000, transcendentals=600_000),
         compiler_params=pltpu.CompilerParams(vmem_limit_bytes=24 << 20),

time: 37.3 us -> 37.6 us (level)
  no operation moved by 1% of the time
where the time goes in v4:
time: 37.6 us; the launch traced here: 37.4 us
  starting transfers between devices  17.9 us (48%)
  Pallas kernels  7.28 us (19%)
  blocking collectives  5.67 us (15%)
  waiting for transfers between devices  5.59 us (15%)
  between operations  0.81 us (2%)
    ppermute x1, starting transfers between devices, layer(): lax.ppermute(jnp.concatenate([own_first] + tail, 0), 'ty', downward(size_y))  11.3 us
    all_gather x1, blocking collectives, layer(): lax.all_gather(send_near, 'tx', axis_index_groups=[[i, i + 1] for i in ra...  5.67 us
    ppermute x1, waiting for transfers between devices, layer(): lax.ppermute(jnp.concatenate([own_last] + tail, 0), 'ty', upward(size_y))  5.59 us
    pallas_call x1, Pallas kernels, layer(): pl.pallas_call(finish_kernel, out_shape=(jax.ShapeDtypeStruct((128, featu...  4.82 us
    ppermute x1, starting transfers between devices, layer(): got_far1 = lax.ppermute(send_far, 'tx', far_pairs(size_x))  4.71 us
    ppermute x1, starting transfers between devices, layer(): lax.ppermute(jnp.concatenate([own_last] + tail, 0), 'ty', upward(size_y))  1.92 us
    pallas_call x1, Pallas kernels, layer(): pl.pallas_call(local_kernel, out_shape=(jax.ShapeDtypeStruct((1024, featu...  1.29 us
    pallas_call x1, Pallas kernels, layer(): pl.pallas_call(pack_kernel, out_shape=(row, row, col, col, jax.ShapeDtype...  1.16 us
  transfers between devices with their start and end apart: 3, of which 1 were waited for; matrix products, arithmetic and copies ran while one was open for 0% of the time, Pallas kernels for 3%

profile of v4, /device:TPU:1, one launch (start us, length us, event | category | flops | bytes accessed | tf_op | source)
XLA Modules:
  0.0 37.4 jit_solution(2892399353555176162)
XLA Ops:
  0.6 0.0 copy-start
  0.6 0.0 copy-start.1
  0.7 0.0 copy-start.3
  0.7 0.0 copy-start.4
  0.7 0.0 copy-start.7
  0.7 1.2 %pack.1 = (bf16[24,512]{1,0:T(8,128)(2,1)S(1)}, bf16[24,512]{1,0:T(8,128)(2,1)S(1)}, bf16[16,512]{1,0:T(8,128)(2,1)S(1)}, bf16[16,512]{1,0:T(8,128)(2,1)S(1)}, s32[8,128]{1,0:T(8,128)S(1)}) custom-call(s32[5]{0:T(128)} %place_hbm.1, bf16[128,512]{1,0:T(8,128)(2,1)} %bitcast.10), custom_call_target="tpu_custom_call" | custom-call | flops 10000000000 | bytes 200000 | tf_op jit(solution)/shard_map/pack/pallas_call | solution.py:263
  1.9 0.0 copy-start.2
  1.9 0.0 copy-start.5
  1.9 0.0 copy-start.6
  1.9 4.7 %collective-permute-start = (bf16[24,512]{1,0:T(8,128)(2,1)S(1)}, bf16[24,512]{1,0:T(8,128)(2,1)S(1)}, u32[]{:S(2)}, u32[]{:S(2)}) collective-permute-start(bf16[24,512]{1,0:T(8,128)(2,1)S(1)} %get-tuple-element.13), channel_id=1, source_target_pairs={{0,496},{16,32},{32,16},{48,64},{64,48},{80,96},{96,80},{112,128},... | collective-permute-start | bytes 73736 | tf_op jit(solution)/shard_map/ppermute | solution.py:280
  6.6 5.7 %all_gather.3.near1_ref = bf16[48,512]{1,0:T(8,128)(2,1)S(1)} all-gather(bf16[24,512]{1,0:T(8,128)(2,1)S(1)} %get-tuple-element.12), channel_id=1, replica_groups={{0,16},{32,48},{64,80},{96,112},{128,144},{160,176},{192,208},{224,240}..., dimensions={0}, use_global_device_ids=true | all-gather | bytes 73728 | tf_op jit(solution)/shard_map/all_gather | solution.py:281
  12.3 0.0 collective-permute-done.far1_ref
  12.3 11.3 %collective-permute-start.2 = (bf16[32,512]{1,0:T(8,128)(2,1)S(1)}, bf16[32,512]{1,0:T(8,128)(2,1)S(1)}, u32[]{:S(2)}, u32[]{:S(2)}) collective-permute-start(bf16[32,512]{1,0:T(8,128)(2,1)S(1)} %get-tuple-element.22), channel_id=1, source_target_pairs={{1,0},{2,1},{3,2},{4,3},{5,4},{6,5},{7,6},{8,7},{9,8},{10,9},{11,1... | collective-permute-start | bytes 98312 | tf_op jit(solution)/shard_map/ppermute | solution.py:300
  23.6 1.9 %collective-permute-start.1 = (bf16[32,512]{1,0:T(8,128)(2,1)S(1)}, bf16[32,512]{1,0:T(8,128)(2,1)S(1)}, u32[]{:S(2)}, u32[]{:S(2)}) collective-permute-start(bf16[32,512]{1,0:T(8,128)(2,1)S(1)} %get-tuple-element.23), channel_id=1, source_target_pairs={{0,1},{1,2},{2,3},{3,4},{4,5},{5,6},{6,7},{7,8},{8,9},{9,10},{10,1... | collective-permute-start | bytes 98312 | tf_op jit(solution)/shard_map/ppermute | solution.py:299
  25.6 0.0 copy-done
  25.6 0.0 copy-done.1
  25.6 0.0 copy-done.3
  25.6 0.0 copy-done.4
  25.6 0.0 copy-done.7
  25.6 1.3 %local.1 = (f32[1024,512]{1,0:T(8,128)S(1)}, bf16[1024,128]{1,0:T(8,128)(2,1)S(1)}, bf16[128,1024]{1,0:T(8,128)(2,1)S(1)}) custom-call(s32[8,128]{1,0:T(8,128)S(1)} %get-tuple-element.16.place_ref, bf16[128,512]{1,0:T(8,128)(2,1)S(1)} %bitcast.11, bf16[1024,512]{1,0:T(8,128)(2,1)S(1)} %bitcast.8, s32[8,128]{1,0:T(8,128)S(1)} %bitcast.17, ...), custom_call_target="tpu_custom_call" | custom-call | flops 1000000000 | bytes 5000000 | tf_op jit(solution)/shard_map/local/pallas_call | solution.py:285
  26.9 0.0 collective-permute-done.2.from_right_ref
  26.9 5.6 %collective-permute-done.1.from_left_ref = bf16[32,512]{1,0:T(8,128)(2,1)S(1)} collective-permute-done((bf16[32,512]{1,0:T(8,128)(2,1)S(1)}, bf16[32,512]{1,0:T(8,128)(2,1)S(1)}, u32[]{:S(2)}, u32[]{:S(2)}) %collective-permute-start.1) | collective-permute-done | bytes 32800 | tf_op jit(solution)/shard_map/ppermute | solution.py:299
  32.5 0.0 copy-done.2
  32.5 0.0 copy-done.5
  32.5 0.0 copy-done.6
  32.5 4.8 %finish.1 = (bf16[128,512]{1,0:T(8,128)(2,1)}, bf16[1024,512]{1,0:T(8,128)(2,1)}) custom-call(bf16[48,512]{1,0:T(8,128)(2,1)S(1)} %all_gather.3.near1_ref, bf16[24,512]{1,0:T(8,128)(2,1)S(1)} %collective-permute-done.far1_ref, bf16[32,512]{1,0:T(8,128)(2,1)S(1)} %collective-permute-done.1.from_left_ref, ...), custom_call_target="tpu_custom_call" | custom-call | flops 1100000000 | bytes 6000000 | tf_op jit(solution)/shard_map/finish/pallas_call | solution.py:301
  (3 shorter events, 0.0 us)
Async XLA Ops:
  0.6 24.9 %copy-start = (bf16[1536,512]{1,0:T(8,128)(2,1)S(1)}, bf16[1536,512]{1,0:T(8,128)(2,1)}, u32[]{:S(2)}) copy-start(bf16[1536,512]{1,0:T(8,128)(2,1)} %w1_ref.3) | copy-start | bytes 4718596
  0.6 24.9 %copy-start.1 = (bf16[1,1,1024,512]{3,2,1,0:T(8,128)(2,1)S(1)}, bf16[1,1,1024,512]{3,2,1,0:T(8,128)(2,1)}, u32[]{:S(2)}) copy-start(bf16[1,1,1024,512]{3,2,1,0:T(8,128)(2,1)} %param.12) | copy-start | bytes 3145732
  0.7 24.9 %copy-start.3 = (bf16[8,16,512]{2,1,0:T(8,128)(2,1)S(1)}, bf16[8,16,512]{2,1,0:T(8,128)(2,1)}, u32[]{:S(2)}) copy-start(bf16[8,16,512]{2,1,0:T(8,128)(2,1)} %param.11) | copy-start | bytes 393220
  0.7 24.9 %copy-start.4 = (s32[1,1,1024]{2,1,0:T(1,128)S(1)}, s32[1,1,1024]{2,1,0:T(1,128)}, u32[]{:S(2)}) copy-start(s32[1,1,1024]{2,1,0:T(1,128)} %param.14) | copy-start | bytes 12292
  0.7 24.9 %copy-start.7 = (s32[1,1,1024]{2,1,0:T(1,128)S(1)}, s32[1,1,1024]{2,1,0:T(1,128)}, u32[]{:S(2)}) copy-start(s32[1,1,1024]{2,1,0:T(1,128)} %param.13) | copy-start | bytes 12292
  1.9 30.7 %copy-start.2 = (bf16[512,512]{1,0:T(8,128)(2,1)S(1)}, bf16[512,512]{1,0:T(8,128)(2,1)}, u32[]{:S(2)}) copy-start(bf16[512,512]{1,0:T(8,128)(2,1)} %w2_ref.1) | copy-start | bytes 1572868
  1.9 30.7 %copy-start.5 = (f32[512]{0:T(512)S(1)}, f32[512]{0:T(512)}, u32[]{:S(2)}) copy-start(f32[512]{0:T(512)} %param.18) | copy-start | bytes 6148
  1.9 30.7 %copy-start.6 = (f32[512]{0:T(512)S(1)}, f32[512]{0:T(512)}, u32[]{:S(2)}) copy-start(f32[512]{0:T(512)} %param.21) | copy-start | bytes 6148
  1.9 10.4 %collective-permute-start = (bf16[24,512]{1,0:T(8,128)(2,1)S(1)}, bf16[24,512]{1,0:T(8,128)(2,1)S(1)}, u32[]{:S(2)}, u32[]{:S(2)}) collective-permute-start(bf16[24,512]{1,0:T(8,128)(2,1)S(1)} %get-tuple-element.13), channel_id=1, source_target_pairs={{0,496},{16,32},{32,16},{48,64},{64,48},{80,96},{96,80},{112,128},... | collective-permute-start | bytes 73736 | tf_op jit(solution)/shard_map/ppermute | solution.py:280
  12.3 14.6 %collective-permute-start.2 = (bf16[32,512]{1,0:T(8,128)(2,1)S(1)}, bf16[32,512]{1,0:T(8,128)(2,1)S(1)}, u32[]{:S(2)}, u32[]{:S(2)}) collective-permute-start(bf16[32,512]{1,0:T(8,128)(2,1)S(1)} %get-tuple-element.22), channel_id=1, source_target_pairs={{1,0},{2,1},{3,2},{4,3},{5,4},{6,5},{7,6},{8,7},{9,8},{10,9},{11,1... | collective-permute-start | bytes 98312 | tf_op jit(solution)/shard_map/ppermute | solution.py:300
  23.6 8.9 %collective-permute-start.1 = (bf16[32,512]{1,0:T(8,128)(2,1)S(1)}, bf16[32,512]{1,0:T(8,128)(2,1)S(1)}, u32[]{:S(2)}, u32[]{:S(2)}) collective-permute-start(bf16[32,512]{1,0:T(8,128)(2,1)S(1)} %get-tuple-element.23), channel_id=1, source_target_pairs={{0,1},{1,2},{2,3},{3,4},{4,5},{5,6},{6,7},{7,8},{8,9},{9,10},{10,1... | collective-permute-start | bytes 98312 | tf_op jit(solution)/shard_map/ppermute | solution.py:299
